TPU v7x, 128 devices: a whole 4x4x4 slice. The times are simulated.
128 devices in a mesh: dom: 32 (over z, y, core), sub: 4 (over x).
Axes of the slice: x: 4, y: 4, z: 4, core: 2. Of those that a mesh axis runs over, the one named last changes fastest.
Arguments:
- node_state: bfloat16 [64, 131072], P(None, ('dom', 'sub')), may hold values from -6 to 6
- edge_state: bfloat16 [64, 393216], P(None, ('dom', 'sub')), may hold values from -6 to 6
- senders: int32 [393216], P(('dom', 'sub')), may hold values from 0 to 2559, as said below
- receivers: int32 [393216], P(('dom', 'sub')), may hold values from 0 to 1023
- send_index: int32 [128, 12, 128], P(('dom', 'sub')), may hold values from -1 to 1023, as said below
- node_cotangent: bfloat16 [64, 131072], P(None, ('dom', 'sub')), may hold values from -6 to 6
- edge_cotangent: bfloat16 [64, 393216], P(None, ('dom', 'sub')), may hold values from -6 to 6
- edge_first: bfloat16 [192, 64], replicated, may hold values from -0.4375 to 0.4375
- edge_bias: float32 [64], replicated, may hold values from -3 to 3
- edge_second: bfloat16 [64, 64], replicated, may hold values from -0.75 to 0.75
- edge_gain: float32 [64], replicated, may hold values from 0.1 to 1.9
- edge_shift: float32 [64], replicated, may hold values from -3 to 3
- node_first: bfloat16 [128, 64], replicated, may hold values from -0.5 to 0.5
- node_bias: float32 [64], replicated, may hold values from -3 to 3
- node_second: bfloat16 [64, 64], replicated, may hold values from -0.75 to 0.75
- node_gain: float32 [64], replicated, may hold values from 0.1 to 1.9
Outputs:
- delta_state: bfloat16 [64, 131072], P(None, ('dom', 'sub'))
- delta_edges: bfloat16 [64, 393216], P(None, ('dom', 'sub'))
- delta_edgefirst: float32 [192, 64], replicated
- delta_edgebias: float32 [64], replicated
- delta_edgesecond: float32 [64, 64], replicated
- delta_edgegain: float32 [64], replicated
- delta_edgeshift: float32 [64], replicated
- delta_nodefirst: float32 [128, 64], replicated
- delta_nodebias: float32 [64], replicated
- delta_nodesecond: float32 [64, 64], replicated
- delta_nodegain: float32 [64], replicated
- delta_nodeshift: float32 [64], replicated
Inputs may be any that keep to these rules, and one draw needn't show every extreme that they name: `send_index`: block k = o * 4 + t of partition p = d * 4 + s lists own cells that p sends to the partition at dom index d + o - 1 and sub index t: live entries first, then -1. Blocks towards a dom index outside the mesh, and block 4 + s, hold only -1; every other block holds 32 to 128 live entries. Some partition receives a full block from every partition that sends to it. `senders`: an entry below 1024 is an own cell. An entry 1024 + k * 128 + j with k = o * 4 + u names ghost slot j of block k: the j-th entry of block o * 4 + s of the partition at dom index d + 1 - o and sub index u, and that entry is live.
All inputs are finite; a program needn't handle non-finite values.
Results may differ from a plain program's by a relative error of at most 0.0095.
Values may be sent and summed in bfloat16 or wider, within the bound.
A program may use at most 64 MiB of HBM per device.

v0:
```python
import math

import jax
import jax.numpy as jnp
from jax import lax
from jax.sharding import Mesh
from jax.sharding import PartitionSpec as P

DOM = ("dom_0", "dom_1", "dom_2")
DOM_SUB = ("dom_0", "dom_1", "dom_2", "sub")


EPSILON = 1e-05


def from_behind(value, axis, steps):
    count = lax.axis_size(axis)
    first, last = (max(0, -steps), min(count, count - steps))
    return lax.ppermute(value, axis, [(source, source + steps) for source in range(first, last)])


def in_blocks(array, dim, peers):
    before, after = (array.shape[:dim], array.shape[dim + 1 :])
    return jnp.moveaxis(array.reshape(*before, peers, -1, *after), dim, 0)


def sum_at_owner(array, axis, dim):
    peers = lax.axis_size(axis)
    tiles = lax.all_to_all(in_blocks(array, dim, peers), axis, 0, 0, tiled=True)
    return jnp.sum(tiles, axis=0)


def sum_in_two_steps(array, axes, dim):
    far, near = axes
    own = sum_at_owner(in_blocks(array, dim, lax.axis_size(far)), near, dim + 1)
    return jnp.sum(lax.all_to_all(own, far, 0, 0, tiled=True), axis=0)


def padded_to(lines, peers):
    spare = -len(lines) % peers
    return jnp.pad(lines, [(0, spare)] + [(0, 0)] * (lines.ndim - 1))


def copy_for_each(array, axis):
    peers = lax.axis_size(axis)
    return lax.all_to_all(
        jnp.broadcast_to(array[None], (peers, *array.shape)), axis, 0, 0, tiled=True
    )


def in_order(tiles, dim):
    tiles = jnp.moveaxis(tiles, 0, dim)
    shape = tiles.shape
    return tiles.reshape(*shape[:dim], shape[dim] * shape[dim + 1], *shape[dim + 2 :])


def whole_of(array, axes, dim):
    far, near = axes
    tiles = copy_for_each(copy_for_each(array, far), near)
    return in_order(tiles.swapaxes(0, 1).reshape(-1, *array.shape), dim)


def total_of(array, axes):
    own = sum_in_two_steps(
        padded_to(array, lax.axis_size(axes[0]) * lax.axis_size(axes[1])), axes, 0
    )
    whole = whole_of(own, axes, 0)
    return whole[: len(array)].reshape(array.shape)


def packed_total(arrays, axis):
    ends = [0]
    for a in arrays:
        ends.append(ends[-1] + a.size)
    running = total_of(jnp.concatenate([a.ravel() for a in arrays]), axis)
    return tuple((running[b:e].reshape(a.shape) for a, b, e in zip(arrays, ends, ends[1:])))


def contract_first(first_operand, second_operand):
    return lax.dot_general(
        first_operand, second_operand, (((0,), (0,)), ((), ())), preferred_element_type=jnp.float32
    )


def contract_last(first_operand, second_operand):
    return lax.dot_general(
        first_operand, second_operand, (((1,), (1,)), ((), ())), preferred_element_type=jnp.float32
    )


def sigmoid_linear(values):
    return values * jax.nn.sigmoid(values)


def sigmoid_slope(values):
    logistic = jax.nn.sigmoid(values)
    return logistic * (1.0 + values * (1.0 - logistic))


def standardize(values):
    centered = values - jnp.mean(values, axis=0, keepdims=True)
    spread = lax.rsqrt(jnp.mean(centered * centered, axis=0, keepdims=True) + EPSILON)
    return (centered * spread, spread)


def normalize_back(upstream, scaled, spread, gain_vector):
    gain_delta = jnp.sum(upstream * scaled, axis=1)
    shift_delta = jnp.sum(upstream, axis=1)
    weighted = upstream * gain_vector[:, None]
    result = spread * (
        weighted
        - jnp.mean(weighted, axis=0, keepdims=True)
        - scaled * jnp.mean(weighted * scaled, axis=0, keepdims=True)
    )
    return (result, gain_delta, shift_delta)


def block_sizes(count, width):
    step = math.gcd(count, 512)
    piece = math.gcd(width, 2048)
    return (step, piece)


def pick_precision(values):
    if values.dtype == jnp.float32:
        return lax.Precision.DEFAULT
    return None


def column_gather(table, index):
    rows, width = table.shape
    count = index.shape[0]
    step, piece = block_sizes(count, width)
    blocks = index.reshape(count // step, step)
    precision = pick_precision(table)

    def one_block(number, result):
        chosen = lax.dynamic_index_in_dim(blocks, number, 0, keepdims=False)
        total = jnp.zeros((rows, step), jnp.float32)
        for begin in range(0, width, piece):
            columns = lax.iota(jnp.int32, piece) + begin
            selector = (columns[:, None] == chosen[None, :]).astype(table.dtype)
            total = total + jnp.dot(
                table[:, begin : begin + piece],
                selector,
                precision=precision,
                preferred_element_type=jnp.float32,
            )
        return lax.dynamic_update_slice_in_dim(result, total.astype(table.dtype), number * step, 1)

    return lax.fori_loop(0, count // step, one_block, jnp.zeros((rows, count), table.dtype))


def column_scatter(values, index, width):
    rows, count = values.shape
    step, piece = block_sizes(count, width)
    blocks = index.reshape(count // step, step)
    precision = pick_precision(values)

    def one_block(number, result):
        chosen = lax.dynamic_index_in_dim(blocks, number, 0, keepdims=False)
        portion = lax.dynamic_slice_in_dim(values, number * step, step, 1)
        pieces = []
        for begin in range(0, width, piece):
            columns = lax.iota(jnp.int32, piece) + begin
            selector = (chosen[:, None] == columns[None, :]).astype(values.dtype)
            pieces.append(
                jnp.dot(portion, selector, precision=precision, preferred_element_type=jnp.float32)
            )
        return result + jnp.concatenate(pieces, axis=1)

    return lax.fori_loop(0, count // step, one_block, jnp.zeros((rows, width), jnp.float32))


def local_backward(
    extended,
    node_state,
    edge_state,
    senders,
    receivers,
    node_cotangent,
    edge_cotangent,
    edge_first,
    edge_bias,
    edge_second,
    edge_gain,
    edge_shift,
    node_first,
    node_bias,
    node_second,
    node_gain,
):
    features, cell_count = node_state.shape
    sender_rows = column_gather(extended, senders)
    receiver_rows = column_gather(node_state, receivers)
    stacked = jnp.concatenate([sender_rows, receiver_rows, edge_state], axis=0)
    edge_linear = contract_first(edge_first, stacked) + edge_bias[:, None]
    edge_active = sigmoid_linear(edge_linear).astype(jnp.bfloat16)
    edge_output = contract_first(edge_second, edge_active)
    edge_scaled, edge_spread = standardize(edge_output)
    message = (edge_scaled * edge_gain[:, None] + edge_shift[:, None]).astype(jnp.bfloat16)
    summed = column_scatter(message, receivers, cell_count)
    node_input = jnp.concatenate([node_state, summed.astype(jnp.bfloat16)], axis=0)
    node_linear = contract_first(node_first, node_input) + node_bias[:, None]
    node_active = sigmoid_linear(node_linear).astype(jnp.bfloat16)
    node_output = contract_first(node_second, node_active)
    node_scaled, node_spread = standardize(node_output)
    upstream = node_cotangent.astype(jnp.float32)
    node_delta, nodegain_delta, nodeshift_delta = normalize_back(
        upstream, node_scaled, node_spread, node_gain
    )
    node_delta = node_delta.astype(jnp.bfloat16)
    nodesecond_delta = contract_last(node_active, node_delta)
    node_hidden = jnp.dot(
        node_second, node_delta, preferred_element_type=jnp.float32
    ) * sigmoid_slope(node_linear)
    nodebias_delta = jnp.sum(node_hidden, axis=1)
    node_hidden = node_hidden.astype(jnp.bfloat16)
    nodefirst_delta = contract_last(node_input, node_hidden)
    node_back = jnp.dot(node_first, node_hidden, preferred_element_type=jnp.float32)
    message_delta = edge_cotangent.astype(jnp.float32) + column_gather(
        node_back[features:], receivers
    )
    edge_delta, edgegain_delta, edgeshift_delta = normalize_back(
        message_delta, edge_scaled, edge_spread, edge_gain
    )
    edge_delta = edge_delta.astype(jnp.bfloat16)
    edgesecond_delta = contract_last(edge_active, edge_delta)
    edge_hidden = jnp.dot(
        edge_second, edge_delta, preferred_element_type=jnp.float32
    ) * sigmoid_slope(edge_linear)
    edgebias_delta = jnp.sum(edge_hidden, axis=1)
    edge_hidden = edge_hidden.astype(jnp.bfloat16)
    edgefirst_delta = contract_last(stacked, edge_hidden)
    edge_back = jnp.dot(edge_first, edge_hidden, preferred_element_type=jnp.float32)
    edge_result = (edge_cotangent.astype(jnp.float32) + edge_back[2 * features :]).astype(
        jnp.bfloat16
    )
    scattered = column_scatter(edge_back[:features], senders, extended.shape[1])
    local_delta = (
        scattered[:, :cell_count]
        + column_scatter(edge_back[features : 2 * features], receivers, cell_count)
        + node_back[:features]
        + upstream
    )
    ghost_delta = scattered[:, cell_count:]
    partials = (
        edgefirst_delta,
        edgebias_delta,
        edgesecond_delta,
        edgegain_delta,
        edgeshift_delta,
        nodefirst_delta,
        nodebias_delta,
        nodesecond_delta,
        nodegain_delta,
        nodeshift_delta,
    )
    return (local_delta, ghost_delta, edge_result, partials)


def on_device(
    node_state,
    edge_state,
    senders,
    receivers,
    send_index,
    node_cotangent,
    edge_cotangent,
    edge_first,
    edge_bias,
    edge_second,
    edge_gain,
    edge_shift,
    node_first,
    node_bias,
    node_second,
    node_gain,
):
    features, cell_count = node_state.shape
    sub_count = lax.axis_size("sub")
    peer_count = 3 * sub_count
    halo_width = send_index.shape[2]
    index_rows = send_index.reshape(peer_count, halo_width)
    live_slots = index_rows >= 0
    safe_index = jnp.where(live_slots, index_rows, 0).reshape(-1)
    picked = column_gather(node_state, safe_index).reshape(features, peer_count, halo_width)
    outgoing = jnp.where(live_slots[None], picked, jnp.zeros_like(picked))
    blocks = outgoing.reshape(features, 3, sub_count, halo_width)
    across = lax.all_to_all(blocks, "sub", split_axis=2, concat_axis=2, tiled=True)
    upper = from_behind(across[:, 0], DOM, -1)
    lower = from_behind(across[:, 2], DOM, 1)
    ghost_rows = jnp.stack([upper, across[:, 1], lower], axis=1).reshape(
        features, peer_count, halo_width
    )
    extended = jnp.concatenate([node_state, ghost_rows.reshape(features, -1)], axis=1)
    local_delta, ghost_delta, edge_result, partials = local_backward(
        extended,
        node_state,
        edge_state,
        senders,
        receivers,
        node_cotangent,
        edge_cotangent,
        edge_first,
        edge_bias,
        edge_second,
        edge_gain,
        edge_shift,
        node_first,
        node_bias,
        node_second,
        node_gain,
    )
    ghost_delta = ghost_delta.reshape(features, peer_count, halo_width)
    grouped = ghost_delta.reshape(features, 3, sub_count, halo_width)
    further = from_behind(grouped[:, 0].astype(jnp.bfloat16), DOM, 1).astype(jnp.float32)
    nearer = from_behind(grouped[:, 2].astype(jnp.bfloat16), DOM, -1).astype(jnp.float32)
    regrouped = jnp.stack([further, grouped[:, 1], nearer], axis=1)
    returned = (
        lax.all_to_all(
            regrouped.astype(jnp.bfloat16), "sub", split_axis=2, concat_axis=2, tiled=True
        )
        .astype(regrouped.dtype)
        .reshape(features, peer_count, halo_width)
    )
    masked = jnp.where(live_slots[None], returned, jnp.zeros_like(returned)).reshape(features, -1)
    local_delta = local_delta + column_scatter(masked, safe_index, cell_count)
    totals = packed_total(
        (
            partials[0],
            partials[1],
            partials[2],
            partials[3],
            partials[4],
            partials[5],
            partials[6],
            partials[7],
            partials[8],
            partials[9],
        ),
        (("dom_0", "dom_1"), ("dom_2", "sub")),
    )
    faces_total = edge_state.shape[1] * lax.axis_size(DOM) * sub_count
    factor = 1.0 / math.sqrt(faces_total)
    (
        edgefirst_sum,
        edgebias_sum,
        edgesecond_sum,
        edgegain_sum,
        edgeshift_sum,
        nodefirst_sum,
        nodebias_sum,
        nodesecond_sum,
        nodegain_sum,
        nodeshift_sum,
    ) = totals
    return (
        local_delta.astype(jnp.bfloat16),
        edge_result,
        edgefirst_sum * factor,
        edgebias_sum * factor,
        edgesecond_sum * factor,
        edgegain_sum * factor,
        edgeshift_sum * factor,
        nodefirst_sum * factor,
        nodebias_sum * factor,
        nodesecond_sum * factor,
        nodegain_sum * factor,
        nodeshift_sum * factor,
    )


def solution(mesh):
    split = Mesh(
        mesh.devices.reshape(4, 4, 2, mesh.shape["sub"]), ("dom_0", "dom_1", "dom_2", "sub")
    )
    in_specs = (
        P(None, DOM_SUB),
        P(None, DOM_SUB),
        P(DOM_SUB),
        P(DOM_SUB),
        P(DOM_SUB, None, None),
        P(None, DOM_SUB),
        P(None, DOM_SUB),
        P(),
        P(),
        P(),
        P(),
        P(),
        P(),
        P(),
        P(),
        P(),
    )
    out_specs = (
        P(None, DOM_SUB),
        P(None, DOM_SUB),
        P(),
        P(),
        P(),
        P(),
        P(),
        P(),
        P(),
        P(),
        P(),
        P(),
    )
    return jax.shard_map(
        on_device, mesh=split, in_specs=in_specs, out_specs=out_specs, check_vma=False
    )
```

profile of v0, /device:TPU:1, one launch (start us, length us, event | category | flops | bytes accessed | tf_op | source)
XLA Modules:
  0.0 186.6 jit_solution(18048583148470305072)
XLA Ops:
  2.2 4.2 %while.108 = (s32[]{:T(128)}, bf16[64,1536]{1,0:T(8,128)(2,1)S(1)}, s32[3,512]{1,0:T(4,128)S(1)}, bf16[64,1024]{1,0:T(8,128)(2,1)}, s32[]{:T(128)}, /*index=5*/s32[]{:T(128)}, s32[]{:T(128)}, s32[]{:T(128)}) while((s32[]{:T(128)}, bf16[64,1536]{1,0:T(8,128)(2,1)S(1)}, s32[3,512]{1,0:T(4,128)S(1)}, bf16[64,1024]{1,0:T(8,128)(2,1)}, s32[]{:T(128)}, ...), condition=%wide.region_1.2_spmd, body=%wide.region_0.1_spmd.sunk | while | flops 67665928 | bytes 202891 | solution.py:151
  7.9 4.8 %all-to-all-start = ((bf16[64,3,4,128]{3,0,1,2:T(8,128)(2,1)}), bf16[64,3,4,128]{3,0,1,2:T(8,128)(2,1)S(1)}, u32[]{:S(2)}, u32[]{:S(2)}) async-start(bf16[64,3,4,128]{3,0,1,2:T(8,128)(2,1)} %copy.70), calls=%async_computation | async-start | bytes 393216 | tf_op jit(solution)/shard_map/all_to_all | solution.py:290
  12.7 5.2 %all-to-all-done = bf16[64,3,4,128]{3,0,1,2:T(8,128)(2,1)S(1)} async-done(((bf16[64,3,4,128]{3,0,1,2:T(8,128)(2,1)}), bf16[64,3,4,128]{3,0,1,2:T(8,128)(2,1)S(1)}, u32[]{:S(2)}, u32[]{:S(2)}) %all-to-all-start) | async-done | bytes 196640 | tf_op jit(solution)/shard_map/all_to_all | solution.py:290
  17.9 5.2 %collective-permute-start.1 = (bf16[64,4,128]{2,0,1:T(8,128)(2,1)S(1)}, bf16[64,4,128]{2,0,1:T(8,128)(2,1)S(1)}, u32[]{:S(2)}, u32[]{:S(2)}) collective-permute-start(bf16[64,4,128]{2,0,1:T(8,128)(2,1)S(1)} %get-tuple-element.869), channel_id=1, source_target_pairs={{0,4},{4,8},{8,12},{12,16},{16,20},{20,24},{24,28},{28,32},{32,36}... | collective-permute-start | bytes 196616 | tf_op jit(solution)/shard_map/ppermute | solution.py:19
  23.1 1.9 %collective-permute-start = (bf16[64,4,128]{2,0,1:T(8,128)(2,1)S(1)}, bf16[64,4,128]{2,0,1:T(8,128)(2,1)S(1)}, u32[]{:S(2)}, u32[]{:S(2)}) collective-permute-start(bf16[64,4,128]{2,0,1:T(8,128)(2,1)S(1)} %get-tuple-element.868), channel_id=1, source_target_pairs={{4,0},{8,4},{12,8},{16,12},{20,16},{24,20},{28,24},{32,28},{36,32}... | collective-permute-start | bytes 196616 | tf_op jit(solution)/shard_map/ppermute | solution.py:19
  25.1 3.0 %while.110 = (s32[]{:T(128)}, bf16[64,3072]{1,0:T(8,128)(2,1)S(1)}, s32[6,512]{1,0:T(8,128)S(1)}, bf16[64,1024]{1,0:T(8,128)(2,1)S(1)}, s32[]{:T(128)}, /*index=5*/s32[]{:T(128)}, s32[]{:T(128)}, s32[]{:T(128)}) while((s32[]{:T(128)}, bf16[64,3072]{1,0:T(8,128)(2,1)S(1)}, s32[6,512]{1,0:T(8,128)S(1)}, bf16[64,1024]{1,0:T(8,128)(2,1)S(1)}, ...), condition=%wide.region_5.6_spmd, body=%wide.region_4.5_spmd.sunk | while | flops 67665928 | bytes 202891 | solution.py:151
  29.0 11.0 %while.109 = (s32[]{:T(128)}, bf16[64,3072]{1,0:T(8,128)(2,1)S(1)}, s32[6,512]{1,0:T(8,128)S(1)}, bf16[64,1024]{1,0:T(8,128)(2,1)S(1)}, bf16[64,1536]{1,0:T(8,12...) while((s32[]{:T(128)}, bf16[64,3072]{1,0:T(8,128)(2,1)S(1)}, s32[6,512]{1,0:T(8,128)S(1)}, ...), condition=%wide.region_3.4_spmd, body=%wide.region_2.3_spmd.sunk | while | flops 169248768 | bytes 1472659 | solution.py:151
  42.7 3.7 %while.112 = (s32[]{:T(128)}, f32[64,1024]{1,0:T(8,128)S(1)}, bf16[64,3072]{1,0:T(8,128)(2,1)S(1)}, s32[6,512]{1,0:T(8,128)S(1)}, s32[]{:T(128)}, /*index=5*/s32[]{:T(128)}, s32[]{:T(128)}, s32[]{:T(128)}) while((s32[]{:T(128)}, f32[64,1024]{1,0:T(8,128)S(1)}, bf16[64,3072]{1,0:T(8,128)(2,1)S(1)}, s32[6,512]{1,0:T(8,128)S(1)}, ...), condition=%wide.region_9.10_spmd.clone, body=%wide.region_8.9_spmd.clone.sunk | while | flops 67764232 | bytes 596117 | solution.py:172
  51.6 3.0 %while.111 = (s32[]{:T(128)}, f32[64,3072]{1,0:T(8,128)S(1)}, s32[6,512]{1,0:T(8,128)S(1)}, bf16[64,1024]{1,0:T(8,128)(2,1)S(1)}, s32[]{:T(128)}, /*index=5*/s32[]{:T(128)}, s32[]{:T(128)}, s32[]{:T(128)}) while((s32[]{:T(128)}, f32[64,3072]{1,0:T(8,128)S(1)}, s32[6,512]{1,0:T(8,128)S(1)}, bf16[64,1024]{1,0:T(8,128)(2,1)S(1)}, s32[]{:T(128)}, ...), condition=%wide.region_15.16_spmd, body=%wide.region_14.15_spmd.sunk | while | flops 67633160 | bytes 268427 | solution.py:151
  61.0 1.5 reshape.184
  64.6 1.6 concatenate.18
  66.2 1.9 %reshape_reshape.16 = f32[16,8,227]{2,1,0:T(8,128)} reshape(f32[29056]{0:T(1024)} %concatenate.18) | data formatting | bytes 232448 | tf_op jit(solution)/shard_map/reshape;reshape | solution.py:24
  68.1 1.6 copy.81
  69.6 3.9 %all-to-all-start.2 = ((f32[8,16,227]{2,1,0:T(8,128)}), f32[8,16,227]{2,1,0:T(8,128)}, u32[]{:S(2)}, u32[]{:S(2)}) async-start(f32[8,16,227]{2,1,0:T(8,128)} %copy.81), calls=%async_computation.2 | async-start | bytes 262144 | tf_op jit(solution)/shard_map/all_to_all | solution.py:29
  74.6 42.4 %while.113 = (s32[]{:T(128)}, f32[64,2560]{1,0:T(8,128)S(1)}, bf16[64,3072]{1,0:T(8,128)(2,1)}, s32[6,512]{1,0:T(8,128)}, s32[]{:T(128)}, /*index=5*/s32[]{:T(128)}, s32[]{:T(128)}, s32[]{:T(128)}) while((s32[]{:T(128)}, f32[64,2560]{1,0:T(8,128)S(1)}, bf16[64,3072]{1,0:T(8,128)(2,1)}, s32[6,512]{1,0:T(8,128)}, s32[]{:T(128)}, ...), condition=%wide.region_19.20_spmd.clone, body=%wide.region_18.19_spmd.clone.sunk | while | flops 169412608 | bytes 2980005 | solution.py:172
  117.2 3.2 %collective-permute-start.2 = (bf16[64,4,128]{2,1,0:T(4,128)(2,1)S(1)}, bf16[64,4,128]{2,1,0:T(4,128)(2,1)S(1)}, u32[]{:S(2)}, u32[]{:S(2)}) collective-permute-start(bf16[64,4,128]{2,1,0:T(4,128)(2,1)S(1)} %get-tuple-element.865), channel_id=1, source_target_pairs={{0,4},{4,8},{8,12},{12,16},{16,20},{20,24},{24,28},{28,32},{32,36}... | collective-permute-start | bytes 196616 | tf_op jit(solution)/shard_map/ppermute | solution.py:19
  120.4 1.9 %collective-permute-start.3 = (bf16[64,4,128]{2,1,0:T(4,128)(2,1)S(1)}, bf16[64,4,128]{2,1,0:T(4,128)(2,1)S(1)}, u32[]{:S(2)}, u32[]{:S(2)}) collective-permute-start(bf16[64,4,128]{2,1,0:T(4,128)(2,1)S(1)} %get-tuple-element.866), channel_id=1, source_target_pairs={{4,0},{8,4},{12,8},{16,12},{20,16},{24,20},{28,24},{32,28},{36,32}... | collective-permute-start | bytes 196616 | tf_op jit(solution)/shard_map/ppermute | solution.py:19
  123.9 9.2 %all-to-all-start.3 = ((f32[16,1,227]{2,1,0:T(1,128)}), f32[16,1,227]{2,1,0:T(1,128)S(1)}, u32[]{:S(2)}, u32[]{:S(2)}) async-start(f32[16,1,227]{2,1,0:T(1,128)} %all_to_all.25), calls=%async_computation.3 | async-start | bytes 32768 | tf_op jit(solution)/shard_map/all_to_all | solution.py:36
  133.1 13.6 %while.114 = (s32[]{:T(128)}, f32[64,1024]{1,0:T(8,128)}, bf16[64,3072]{1,0:T(8,128)(2,1)}, s32[6,512]{1,0:T(8,128)S(1)}, s32[]{:T(128)}, /*index=5*/s32[]{:T(128)}, s32[]{:T(128)}, s32[]{:T(128)}) while((s32[]{:T(128)}, f32[64,1024]{1,0:T(8,128)}, bf16[64,3072]{1,0:T(8,128)(2,1)}, s32[6,512]{1,0:T(8,128)S(1)}, s32[]{:T(128)}, ...), condition=%wide.region_21.22_spmd.clone, body=%wide.region_20.21_spmd.clone.sunk | while | flops 67764232 | bytes 596117 | solution.py:172
  133.2 2.1 %fusion.198 = f32[64,1024]{1,0:T(8,128)} fusion(s32[512]{0:T(512)S(1)} %bitcast.164, f32[64,1024]{1,0:T(8,128)} %get-tuple-element.1281, bf16[64,3072]{1,0:T(8,128)(2,1)} %get-tuple-element.1290, s32[]{:T(128)S(6)} %select_n.137, pred[]{:T(512)S(6)} %compare.14), kind=kOutput, calls=%fused_computation.96.clone.1 | convolution fusion | flops 67764224 | bytes 591877 | tf_op jit(solution)/shard_map/while/body/eval_jaxpr/dot_general | solution.py:168
  135.3 2.3 %fusion.198 = f32[64,1024]{1,0:T(8,128)} fusion(s32[512]{0:T(512)S(1)} %bitcast.164, f32[64,1024]{1,0:T(8,128)} %get-tuple-element.1281, bf16[64,3072]{1,0:T(8,128)(2,1)} %get-tuple-element.1290, s32[]{:T(128)S(6)} %select_n.137, pred[]{:T(512)S(6)} %compare.14), kind=kOutput, calls=%fused_computation.96.clone.1 | convolution fusion | flops 67764224 | bytes 591877 | tf_op jit(solution)/shard_map/while/body/eval_jaxpr/dot_general | solution.py:168
  137.6 2.3 %fusion.198 = f32[64,1024]{1,0:T(8,128)} fusion(s32[512]{0:T(512)S(1)} %bitcast.164, f32[64,1024]{1,0:T(8,128)} %get-tuple-element.1281, bf16[64,3072]{1,0:T(8,128)(2,1)} %get-tuple-element.1290, s32[]{:T(128)S(6)} %select_n.137, pred[]{:T(512)S(6)} %compare.14), kind=kOutput, calls=%fused_computation.96.clone.1 | convolution fusion | flops 67764224 | bytes 591877 | tf_op jit(solution)/shard_map/while/body/eval_jaxpr/dot_general | solution.py:168
  139.9 2.3 %fusion.198 = f32[64,1024]{1,0:T(8,128)} fusion(s32[512]{0:T(512)S(1)} %bitcast.164, f32[64,1024]{1,0:T(8,128)} %get-tuple-element.1281, bf16[64,3072]{1,0:T(8,128)(2,1)} %get-tuple-element.1290, s32[]{:T(128)S(6)} %select_n.137, pred[]{:T(512)S(6)} %compare.14), kind=kOutput, calls=%fused_computation.96.clone.1 | convolution fusion | flops 67764224 | bytes 591877 | tf_op jit(solution)/shard_map/while/body/eval_jaxpr/dot_general | solution.py:168
  142.1 2.3 %fusion.198 = f32[64,1024]{1,0:T(8,128)} fusion(s32[512]{0:T(512)S(1)} %bitcast.164, f32[64,1024]{1,0:T(8,128)} %get-tuple-element.1281, bf16[64,3072]{1,0:T(8,128)(2,1)} %get-tuple-element.1290, s32[]{:T(128)S(6)} %select_n.137, pred[]{:T(512)S(6)} %compare.14), kind=kOutput, calls=%fused_computation.96.clone.1 | convolution fusion | flops 67764224 | bytes 591877 | tf_op jit(solution)/shard_map/while/body/eval_jaxpr/dot_general | solution.py:168
  144.4 2.3 %fusion.198 = f32[64,1024]{1,0:T(8,128)} fusion(s32[512]{0:T(512)S(1)} %bitcast.164, f32[64,1024]{1,0:T(8,128)} %get-tuple-element.1281, bf16[64,3072]{1,0:T(8,128)(2,1)} %get-tuple-element.1290, s32[]{:T(128)S(6)} %select_n.137, pred[]{:T(512)S(6)} %compare.14), kind=kOutput, calls=%fused_computation.96.clone.1 | convolution fusion | flops 67764224 | bytes 591877 | tf_op jit(solution)/shard_map/while/body/eval_jaxpr/dot_general | solution.py:168
  147.4 6.6 %all-to-all-start.4 = ((f32[16,1,227]{2,1,0:T(1,128)}), f32[16,1,227]{2,1,0:T(1,128)S(1)}, u32[]{:S(2)}, u32[]{:S(2)}) async-start(f32[16,1,227]{2,1,0:T(1,128)} %broadcast_in_dim.148), calls=%async_computation.4 | async-start | bytes 32768 | tf_op jit(solution)/shard_map/all_to_all | solution.py:46
  154.9 5.5 %all-to-all-done.4 = f32[16,1,227]{2,1,0:T(1,128)S(1)} async-done(((f32[16,1,227]{2,1,0:T(1,128)}), f32[16,1,227]{2,1,0:T(1,128)S(1)}, u32[]{:S(2)}, u32[]{:S(2)}) %all-to-all-start.4) | async-done | bytes 14560 | tf_op jit(solution)/shard_map/all_to_all | solution.py:46
  160.4 4.4 %all-to-all-start.1 = ((bf16[64,3,4,128]{3,0,1,2:T(8,128)(2,1)}), bf16[64,3,4,128]{3,0,1,2:T(8,128)(2,1)S(1)}, u32[]{:S(2)}, u32[]{:S(2)}) async-start(bf16[64,3,4,128]{3,0,1,2:T(8,128)(2,1)} %copy.77), calls=%async_computation.1 | async-start | bytes 393216 | tf_op jit(solution)/shard_map/all_to_all | solution.py:321
  164.8 1.9 %fusion.78 = bf16[64,3072]{1,0:T(8,128)(2,1)} fusion(bf16[64,3072]{1,0:T(8,128)(2,1)S(1)} %copy-done.2, f32[192,3072]{1,0:T(8,128)} %copy-done.1), kind=kLoop, calls=%fused_computation.120 | loop fusion | flops 589824 | bytes 1572864 | tf_op jit(solution)/shard_map/convert_element_type | solution.py:236
  166.8 3.2 %all-to-all-done.1 = bf16[64,3,4,128]{3,0,1,2:T(8,128)(2,1)S(1)} async-done(((bf16[64,3,4,128]{3,0,1,2:T(8,128)(2,1)}), bf16[64,3,4,128]{3,0,1,2:T(8,128)(2,1)S(1)}, u32[]{:S(2)}, u32[]{:S(2)}) %all-to-all-start.1) | async-done | bytes 196640 | tf_op jit(solution)/shard_map/all_to_all | solution.py:321
  170.7 7.4 %all-to-all-start.5 = ((f32[8,16,227]{2,1,0:T(8,128)}), f32[8,16,227]{2,1,0:T(8,128)S(1)}, u32[]{:S(2)}, u32[]{:S(2)}) async-start(f32[8,16,227]{2,1,0:T(8,128)} %broadcast_in_dim.150), calls=%async_computation.5 | async-start | bytes 262144 | tf_op jit(solution)/shard_map/all_to_all | solution.py:46
  178.4 4.1 %while.115 = (s32[]{:T(128)}, f32[64,1024]{1,0:T(8,128)S(1)}, bf16[64,1536]{1,0:T(8,128)(2,1)S(1)}, s32[3,512]{1,0:T(4,128)}, s32[]{:T(128)}, /*index=5*/s32[]{:T(128)}, s32[]{:T(128)}, s32[]{:T(128)}) while((s32[]{:T(128)}, f32[64,1024]{1,0:T(8,128)S(1)}, bf16[64,1536]{1,0:T(8,128)(2,1)S(1)}, s32[3,512]{1,0:T(4,128)}, ...), condition=%wide.region_23.24_spmd.clone, body=%wide.region_22.23_spmd.clone.sunk | while | flops 67764232 | bytes 596117 | solution.py:172
  (324 shorter events, 98.9 us)
Async XLA Ops:
  0.6 39.6 %copy-start = (bf16[192,64]{0,1:T(8,128)(2,1)S(1)}, bf16[192,64]{0,1:T(8,128)(2,1)}, u32[]{:S(2)}) copy-start(bf16[192,64]{0,1:T(8,128)(2,1)} %param.39) | copy-start | bytes 73732
  2.1 5.0 %copy-start.14 = (pred[12,128]{1,0:T(8,128)(4,1)}, pred[12,128]{1,0:T(8,128)(4,1)S(1)}, u32[]{:S(2)}) copy-start(pred[12,128]{1,0:T(8,128)(4,1)S(1)} %compare_reduce_fusion) | copy-start | bytes 4612
  2.2 10.6 %copy-start.19 = (s32[3072]{0:T(1024)S(1)}, s32[3072]{0:T(1024)}, u32[]{:S(2)}) copy-start(s32[3072]{0:T(1024)} %param.35) | copy-start | bytes 36868
  7.0 18.1 %copy-start.24 = (bf16[64,1024]{1,0:T(8,128)(2,1)S(1)}, bf16[64,1024]{1,0:T(8,128)(2,1)}, u32[]{:S(2)}) copy-start(bf16[64,1024]{1,0:T(8,128)(2,1)} %get-tuple-element.1316) | copy-start | bytes 393220
  7.9 10.0 %all-to-all-start = ((bf16[64,3,4,128]{3,0,1,2:T(8,128)(2,1)}), bf16[64,3,4,128]{3,0,1,2:T(8,128)(2,1)S(1)}, u32[]{:S(2)}, u32[]{:S(2)}) async-start(bf16[64,3,4,128]{3,0,1,2:T(8,128)(2,1)} %copy.70), calls=%async_computation | async-start | bytes 393216 | tf_op jit(solution)/shard_map/all_to_all | solution.py:290
  17.9 10.3 %collective-permute-start.1 = (bf16[64,4,128]{2,0,1:T(8,128)(2,1)S(1)}, bf16[64,4,128]{2,0,1:T(8,128)(2,1)S(1)}, u32[]{:S(2)}, u32[]{:S(2)}) collective-permute-start(bf16[64,4,128]{2,0,1:T(8,128)(2,1)S(1)} %get-tuple-element.869), channel_id=1, source_target_pairs={{0,4},{4,8},{8,12},{12,16},{16,20},{20,24},{24,28},{28,32},{32,36}... | collective-permute-start | bytes 196616 | tf_op jit(solution)/shard_map/ppermute | solution.py:19
  23.1 5.6 %collective-permute-start = (bf16[64,4,128]{2,0,1:T(8,128)(2,1)S(1)}, bf16[64,4,128]{2,0,1:T(8,128)(2,1)S(1)}, u32[]{:S(2)}, u32[]{:S(2)}) collective-permute-start(bf16[64,4,128]{2,0,1:T(8,128)(2,1)S(1)} %get-tuple-element.868), channel_id=1, source_target_pairs={{4,0},{8,4},{12,8},{16,12},{20,16},{24,20},{28,24},{32,28},{36,32}... | collective-permute-start | bytes 196616 | tf_op jit(solution)/shard_map/ppermute | solution.py:19
  25.1 3.1 %copy-start.20 = (s32[3072]{0:T(1024)S(1)}, s32[3072]{0:T(1024)}, u32[]{:S(2)}) copy-start(s32[3072]{0:T(1024)} %param.34) | copy-start | bytes 36868
  29.0 11.1 %copy-start.9 = (bf16[64,3072]{1,0:T(8,128)(2,1)S(1)}, bf16[64,3072]{1,0:T(8,128)(2,1)}, u32[]{:S(2)}) copy-start(bf16[64,3072]{1,0:T(8,128)(2,1)} %param.33) | copy-start | bytes 1179652
  40.1 2.0 %copy-start.13 = (s32[6,512]{1,0:T(8,128)}, s32[6,512]{1,0:T(8,128)S(1)}, u32[]{:S(2)}) copy-start(s32[6,512]{1,0:T(8,128)S(1)} %get-tuple-element.1305) | copy-start | bytes 36868
  40.8 1.3 copy-start.3
  40.8 1.3 copy-start.16
  40.8 1.8 copy-start.21
  40.8 1.8 copy-start.23
  42.7 3.8 %copy-start.18 = (bf16[128,64]{0,1:T(8,128)(2,1)S(1)}, bf16[128,64]{0,1:T(8,128)(2,1)}, u32[]{:S(2)}) copy-start(bf16[128,64]{0,1:T(8,128)(2,1)} %param.44) | copy-start | bytes 49156
  42.7 3.8 %copy-start.26 = (f32[64]{0:T(128)S(1)}, f32[64]{0:T(128)}, u32[]{:S(2)}) copy-start(f32[64]{0:T(128)} %param.45) | copy-start | bytes 772
  42.7 4.0 %copy-start.17 = (bf16[64,64]{1,0:T(8,128)(2,1)S(1)}, bf16[64,64]{1,0:T(8,128)(2,1)}, u32[]{:S(2)}) copy-start(bf16[64,64]{1,0:T(8,128)(2,1)} %param.46) | copy-start | bytes 24580
  51.6 3.0 %copy-start.2 = (bf16[64,3072]{1,0:T(8,128)(2,1)S(1)}, bf16[64,3072]{1,0:T(8,128)(2,1)}, u32[]{:S(2)}) copy-start(bf16[64,3072]{1,0:T(8,128)(2,1)} %param.38) | copy-start | bytes 1179652
  57.2 1.3 copy-start.4
  59.5 15.1 %copy-start.1 = (f32[192,3072]{1,0:T(8,128)}, f32[192,3072]{1,0:T(8,128)S(1)}, u32[]{:S(2)}) copy-start(f32[192,3072]{1,0:T(8,128)S(1)} %convolution_bitcast_fusion) | copy-start | bytes 7077892
  69.6 52.7 %all-to-all-start.2 = ((f32[8,16,227]{2,1,0:T(8,128)}), f32[8,16,227]{2,1,0:T(8,128)}, u32[]{:S(2)}, u32[]{:S(2)}) async-start(f32[8,16,227]{2,1,0:T(8,128)} %copy.81), calls=%async_computation.2 | async-start | bytes 262144 | tf_op jit(solution)/shard_map/all_to_all | solution.py:29
  117.2 36.8 %collective-permute-start.2 = (bf16[64,4,128]{2,1,0:T(4,128)(2,1)S(1)}, bf16[64,4,128]{2,1,0:T(4,128)(2,1)S(1)}, u32[]{:S(2)}, u32[]{:S(2)}) collective-permute-start(bf16[64,4,128]{2,1,0:T(4,128)(2,1)S(1)} %get-tuple-element.865), channel_id=1, source_target_pairs={{0,4},{4,8},{8,12},{12,16},{16,20},{20,24},{24,28},{28,32},{32,36}... | collective-permute-start | bytes 196616 | tf_op jit(solution)/shard_map/ppermute | solution.py:19
  120.4 33.6 %collective-permute-start.3 = (bf16[64,4,128]{2,1,0:T(4,128)(2,1)S(1)}, bf16[64,4,128]{2,1,0:T(4,128)(2,1)S(1)}, u32[]{:S(2)}, u32[]{:S(2)}) collective-permute-start(bf16[64,4,128]{2,1,0:T(4,128)(2,1)S(1)} %get-tuple-element.866), channel_id=1, source_target_pairs={{4,0},{8,4},{12,8},{16,12},{20,16},{24,20},{28,24},{32,28},{36,32}... | collective-permute-start | bytes 196616 | tf_op jit(solution)/shard_map/ppermute | solution.py:19
  123.9 22.8 %all-to-all-start.3 = ((f32[16,1,227]{2,1,0:T(1,128)}), f32[16,1,227]{2,1,0:T(1,128)S(1)}, u32[]{:S(2)}, u32[]{:S(2)}) async-start(f32[16,1,227]{2,1,0:T(1,128)} %all_to_all.25), calls=%async_computation.3 | async-start | bytes 32768 | tf_op jit(solution)/shard_map/all_to_all | solution.py:36
  146.7 31.6 %copy-start.15 = (pred[12,128]{1,0:T(8,128)(4,1)S(1)}, pred[12,128]{1,0:T(8,128)(4,1)}, u32[]{:S(2)}) copy-start(pred[12,128]{1,0:T(8,128)(4,1)} %copy-done.14) | copy-start | bytes 4612
  147.4 13.1 %all-to-all-start.4 = ((f32[16,1,227]{2,1,0:T(1,128)}), f32[16,1,227]{2,1,0:T(1,128)S(1)}, u32[]{:S(2)}, u32[]{:S(2)}) async-start(f32[16,1,227]{2,1,0:T(1,128)} %broadcast_in_dim.148), calls=%async_computation.4 | async-start | bytes 32768 | tf_op jit(solution)/shard_map/all_to_all | solution.py:46
  154.0 24.3 %copy-start.10 = (f32[64,1024]{1,0:T(8,128)S(1)}, f32[64,1024]{1,0:T(8,128)}, u32[]{:S(2)}) copy-start(f32[64,1024]{1,0:T(8,128)} %custom-call.3) | copy-start | bytes 786436
  160.4 9.6 %all-to-all-start.1 = ((bf16[64,3,4,128]{3,0,1,2:T(8,128)(2,1)}), bf16[64,3,4,128]{3,0,1,2:T(8,128)(2,1)S(1)}, u32[]{:S(2)}, u32[]{:S(2)}) async-start(bf16[64,3,4,128]{3,0,1,2:T(8,128)(2,1)} %copy.77), calls=%async_computation.1 | async-start | bytes 393216 | tf_op jit(solution)/shard_map/all_to_all | solution.py:321
  170.7 12.6 %all-to-all-start.5 = ((f32[8,16,227]{2,1,0:T(8,128)}), f32[8,16,227]{2,1,0:T(8,128)S(1)}, u32[]{:S(2)}, u32[]{:S(2)}) async-start(f32[8,16,227]{2,1,0:T(8,128)} %broadcast_in_dim.150), calls=%async_computation.5 | async-start | bytes 262144 | tf_op jit(solution)/shard_map/all_to_all | solution.py:46
  178.4 4.1 %copy-start.6 = (f32[128,1024]{1,0:T(8,128)S(1)}, f32[128,1024]{1,0:T(8,128)}, u32[]{:S(2)}) copy-start(f32[128,1024]{1,0:T(8,128)} %copy-done.5) | copy-start | bytes 1572868
  178.4 4.1 %copy-start.8 = (bf16[64,1024]{1,0:T(8,128)(2,1)S(1)}, bf16[64,1024]{1,0:T(8,128)(2,1)}, u32[]{:S(2)}) copy-start(bf16[64,1024]{1,0:T(8,128)(2,1)} %param.37) | copy-start | bytes 393220
  178.4 4.1 %copy-start.11 = (f32[64,1024]{1,0:T(8,128)S(1)}, f32[64,1024]{1,0:T(8,128)}, u32[]{:S(2)}) copy-start(f32[64,1024]{1,0:T(8,128)} %get-tuple-element.665) | copy-start | bytes 786436
  (6 other events, 5.0 us)
where the time goes:
time: 190 us; the launch traced here: 187 us
  matrix products  82.8 us (44%)
  starting transfers between devices  48.7 us (26%)
  local copies, waits for them, and re-layouts  26.8 us (14%)
  waiting for transfers between devices  14.4 us (8%)
  other arithmetic  10.9 us (6%)
    dot_general x45, matrix products, one_block(): jnp.dot(portion, selector, precision=precision, preferred_element_type=jn...  55.1 us
    dot_general x45, matrix products, one_block(): jnp.dot(table[:, begin:begin + piece], selector, precision=precision, pre...  20.1 us
    all_to_all x2, starting transfers between devices, copy_for_each(): lax.all_to_all(jnp.broadcast_to(array[None], (peers, *array.shape)), axis...  14 us
    ppermute x4, starting transfers between devices, from_behind(): lax.ppermute(value, axis, [(source, source + steps) for source in range(f...  12.3 us
    all_to_all x1, starting transfers between devices, sum_in_two_steps(): return jnp.sum(lax.all_to_all(own, far, 0, 0, tiled=True), axis=0)  9.24 us
    dynamic_slice x42, local copies, waits for them, and re-layouts, one_block(): chosen = lax.dynamic_index_in_dim(blocks, number, 0, keepdims=False)  6.82 us
    all_to_all x2, waiting for transfers between devices, copy_for_each(): lax.all_to_all(jnp.broadcast_to(array[None], (peers, *array.shape)), axis...  5.54 us
    all_to_all x1, waiting for transfers between devices, on_device(): lax.all_to_all(blocks, 'sub', split_axis=2, concat_axis=2, tiled=True)  5.17 us
  transfers between devices with their start and end apart: 10, of which 4 were waited for; matrix products, arithmetic and copies ran while one was open for 37% of the time, Pallas kernels for 0%

commit v1 on v0

v1 whole, which is shorter than its diff:
```python
import math

import jax
import jax.numpy as jnp
from jax import lax
from jax.experimental import pallas as pl
from jax.experimental.pallas import tpu as pltpu
from jax.sharding import Mesh
from jax.sharding import PartitionSpec as P

AXES = ("z", "y", "core", "sub")
MESH = pl.DeviceIdType.MESH
EPSILON = 1e-05
D = 64
NF = 3072
NC = 1024
NB = 12
HALO = 128
BLK = 512
bf16 = jnp.bfloat16
f32 = jnp.float32
FACTOR = 1.0 / math.sqrt(393216)


def mm(a, b):
    return jnp.dot(a, b, preferred_element_type=f32)


def mm_last(a, b):
    return lax.dot_general(a, b, (((1,), (1,)), ((), ())), preferred_element_type=f32)


def split_index(row):
    return row & 255, row >> 8


def sub_iota(width):
    return lax.broadcasted_iota(jnp.int32, (256, width), 0).astype(f32).astype(bf16)


def selector(lo, hi, tile, iota):
    key = jnp.where(hi == tile, lo, -1).astype(f32).astype(bf16)
    return jnp.where(iota == key, bf16(1), bf16(0))


def columns_of(lo, hi):
    width = lo.shape[1]
    row = lax.broadcasted_iota(jnp.int32, (8, width), 0)
    stacked = jnp.where(row == 0, lo, jnp.where(row == 1, hi, 0)).astype(f32)
    sub = lax.broadcasted_iota(jnp.int32, (8, 256), 0)
    lane = lax.broadcasted_iota(jnp.int32, (8, 256), 1)
    chooser = jnp.where(((sub == 0) & (lane < 128)) | ((sub == 1) & (lane >= 128)), 1.0, 0.0)
    out = lax.dot_general(
        stacked, chooser, (((0,), (0,)), ((), ())), preferred_element_type=f32
    )
    return out.astype(bf16)


def lane_iotas():
    lane = lax.broadcasted_iota(jnp.int32, (1, 128), 1)
    return lane.astype(f32).astype(bf16), (lane + 128).astype(f32).astype(bf16)


def selector_t(lo, hi, tile, iotas):
    key = jnp.where(hi == bf16(tile), lo, bf16(-1))
    return jnp.concatenate(
        [jnp.where(key == lanes, bf16(1), bf16(0)) for lanes in iotas], axis=1
    )


def column_of(row):
    sub = lax.broadcasted_iota(jnp.int32, (D, D), 0)
    lane = lax.broadcasted_iota(jnp.int32, (D, D), 1)
    col = jnp.sum(jnp.where(sub == lane, row, 0.0), axis=1, keepdims=True)
    return jnp.broadcast_to(col, (D, 128))


def wide(col, width):
    return jnp.concatenate([col] * (width // 128), axis=1)


def fold_lanes(values):
    total = values[:, 0:128]
    for begin in range(128, values.shape[1], 128):
        total = total + values[:, begin : begin + 128]
    return total


def mean_rows(values):
    return jnp.sum(values, axis=0, keepdims=True) * (1.0 / D)


def logistic(values):
    return 0.5 * jnp.tanh(0.5 * values) + 0.5


def standardize(values):
    centered = values - mean_rows(values)
    spread = lax.rsqrt(mean_rows(centered * centered) + EPSILON)
    return centered * spread, spread


def normalize_back(upstream, scaled, spread, gain):
    weighted = upstream * gain
    return spread * (weighted - mean_rows(weighted) - scaled * mean_rows(weighted * scaled))


def make_kernel(comm):
    def kernel(
        ns, es, snd, rcv, six, nct, ect, w1, b1, w2, eg, esh, nw1, nb1, nw2, ng,
        dstate, dedges, o_w1, o_b1, o_w2, o_eg, o_es, o_nw1, o_nb1, o_nw2, o_ng, o_ns,
        stk, slope, scl, spr, msg, ehd, col_s, col_r, col_p,
        sendb, ghost, gsend, gback, nin, nh2, nbr, own, acc, gt, gsb,
        vec, sums, grads, rs_buf, ex_buf, ag_buf, w1t, w2t, nw1t, nw2t,
        sem_fs, sem_fr, sem_bs, sem_br, sem_rs, sem_rr, sem_es, sem_er, sem_as, sem_ar,
    ):
        if comm:
            z = lax.axis_index("z")
            y = lax.axis_index("y")
            core = lax.axis_index("core")
            s = lax.axis_index("sub")
            d = z * 8 + y * 2 + core
            a = z * 2 + core
            b = y * 4 + s

            def row_peer(step, r):
                dd = lax.rem(d + (step + 32), 32)
                return (
                    lax.div(dd, 8),
                    lax.rem(lax.div(dd, 2), 4),
                    lax.rem(dd, 2),
                    lax.rem(s + r, 4),
                )

            def a_peer(j):
                other = lax.rem(a + j, 8)
                return other, (lax.div(other, 2), y, lax.rem(other, 2), s)

            def b_peer(j):
                other = lax.rem(b + j, 16)
                return other, (z, lax.div(other, 4), core, lax.rem(other, 4))

            halo_pairs = [(o, r) for o in range(3) for r in range(4) if not (o == 1 and r == 0)]
            barrier = pltpu.get_barrier_semaphore()
            peers = [row_peer(o - 1, r) for o, r in halo_pairs]
            peers += [a_peer(j)[1] for j in range(1, 8)] + [b_peer(j)[1] for j in range(1, 16)]
            for peer in peers:
                pl.semaphore_signal(barrier, inc=1, device_id=peer, device_id_type=MESH)
        else:
            s = 0

        iota = sub_iota(256)
        iota2 = jnp.concatenate([iota, iota], axis=1)
        iotas = lane_iotas()

        for pair in range(NB // 2):
            row = jnp.concatenate([six[2 * pair : 2 * pair + 1, :], six[2 * pair + 1 : 2 * pair + 2, :]], axis=1)
            lo, hi = split_index(row)
            picked = jnp.zeros((D, 256), f32)
            for tile in range(4):
                picked = picked + mm(
                    ns[:, 256 * tile : 256 * tile + 256], selector(lo, hi, tile, iota)
                )
            picked = picked.astype(bf16)
            sendb[2 * pair] = picked[:, :HALO]
            sendb[2 * pair + 1] = picked[:, HALO:]
            col_p[256 * pair : 256 * pair + 256, :] = columns_of(lo, hi)

        ghost[4 + s] = jnp.zeros((D, HALO), bf16)
        gback[4 + s] = jnp.zeros((D, HALO), bf16)

        forward = []
        backward = []
        if comm:
            pl.semaphore_wait(barrier, len(peers))
            for number, (o, r) in enumerate(halo_pairs):
                t = lax.rem(s + r, 4)
                forward.append(
                    pltpu.make_async_remote_copy(
                        src_ref=sendb.at[o * 4 + t],
                        dst_ref=ghost.at[o * 4 + s],
                        send_sem=sem_fs.at[number],
                        recv_sem=sem_fr.at[o * 4 + s],
                        device_id=row_peer(o - 1, r),
                        device_id_type=MESH,
                    )
                )
            for copy in forward:
                copy.start()

        vec[0] = column_of(b1[...])
        vec[1] = column_of(eg[...])
        vec[2] = column_of(esh[...])
        vec[3] = column_of(nb1[...])
        vec[4] = column_of(ng[...])
        w1t[...] = w1[...].astype(f32).T.astype(bf16)
        w2t[...] = w2[...].astype(f32).T.astype(bf16)
        nw1t[...] = nw1[...].astype(f32).T.astype(bf16)
        nw2t[...] = nw2[...].astype(f32).T.astype(bf16)
        sums[...] = jnp.zeros_like(sums)
        stk[128:192, :] = es[...]
        nin[0:64, :] = ns[...]

        def gather_own(i, carry):
            at = pl.ds(pl.multiple_of(i * BLK, BLK), BLK)
            for index, begin, cols in ((snd, 0, col_s), (rcv, 64, col_r)):
                lo, hi = split_index(index[:, at])
                total = jnp.zeros((D, BLK), f32)
                for tile in range(4):
                    total = total + mm(
                        ns[:, 256 * tile : 256 * tile + 256], selector(lo, hi, tile, iota2)
                    )
                stk[begin : begin + 64, at] = total.astype(bf16)
                cols[at, :] = columns_of(lo, hi)
            return carry

        lax.fori_loop(0, NF // BLK, gather_own, 0)

        if comm:
            for o, r in halo_pairs:
                t = lax.rem(s + r, 4)
                pltpu.make_async_remote_copy(
                    src_ref=sendb.at[o * 4 + t],
                    dst_ref=ghost.at[o * 4 + t],
                    send_sem=sem_fs.at[0],
                    recv_sem=sem_fr.at[o * 4 + t],
                    device_id=row_peer(o - 1, r),
                    device_id_type=MESH,
                ).wait_recv()

        def forward_faces(i, carry):
            at = pl.ds(pl.multiple_of(i * BLK, BLK), BLK)
            lo, hi = split_index(snd[:, at])
            total = stk[0:64, at].astype(f32)
            for pair in range(NB // 2):
                table = jnp.concatenate([ghost[2 * pair], ghost[2 * pair + 1]], axis=1)
                total = total + mm(table, selector(lo, hi, 4 + pair, iota2))
            stk[0:64, at] = total.astype(bf16)
            linear = mm(w1t[...], stk[0:192, at]) + wide(vec[0], BLK)
            gate = logistic(linear)
            active = (linear * gate).astype(bf16)
            stk[192:256, at] = active
            slope[:, at] = gate * (1.0 + linear * (1.0 - gate))
            scaled, spread = standardize(mm(w2t[...], active))
            scl[:, at] = scaled
            spr[:, at] = spread
            msg[:, at] = (scaled * wide(vec[1], BLK) + wide(vec[2], BLK)).astype(bf16)
            return carry

        lax.fori_loop(0, NF // BLK, forward_faces, 0)

        acc[:, 0:NC] = jnp.zeros((D, NC), f32)

        def sum_messages(i, carry):
            at = pl.ds(pl.multiple_of(i * BLK, BLK), BLK)
            lo, hi = col_r[at, 0:128], col_r[at, 128:256]
            part = msg[:, at]
            for tile in range(4):
                where = slice(256 * tile, 256 * tile + 256)
                acc[:, where] += mm(part, selector_t(lo, hi, tile, iotas))
            return carry

        lax.fori_loop(0, NF // BLK, sum_messages, 0)

        def cells(i, carry):
            at = pl.ds(pl.multiple_of(i * BLK, BLK), BLK)
            nin[64:128, at] = acc[:, at].astype(bf16)
            linear = mm(nw1t[...], nin[0:128, at]) + wide(vec[3], BLK)
            gate = logistic(linear)
            active = (linear * gate).astype(bf16)
            nin[128:192, at] = active
            scaled, spread = standardize(mm(nw2t[...], active))
            upstream = nct[:, at].astype(f32)
            sums[4] += fold_lanes(upstream * scaled)
            sums[5] += fold_lanes(upstream)
            delta = normalize_back(upstream, scaled, spread, wide(vec[4], BLK)).astype(bf16)
            nh2[0:64, at] = delta
            hidden = mm(nw2[...], delta) * (gate * (1.0 + linear * (1.0 - gate)))
            sums[3] += fold_lanes(hidden)
            hidden = hidden.astype(bf16)
            nh2[64:128, at] = hidden
            back = mm(nw1[...], hidden)
            own[:, at] = back[0:64] + upstream
            nbr[:, at] = back[64:128].astype(bf16)
            return carry

        lax.fori_loop(0, NC // BLK, cells, 0)

        def backward_faces(i, carry):
            at = pl.ds(pl.multiple_of(i * BLK, BLK), BLK)
            lo, hi = split_index(rcv[:, at])
            cotangent = ect[:, at].astype(f32)
            upstream = cotangent
            for tile in range(4):
                upstream = upstream + mm(
                    nbr[:, 256 * tile : 256 * tile + 256], selector(lo, hi, tile, iota2)
                )
            scaled = scl[:, at]
            sums[1] += fold_lanes(upstream * scaled)
            sums[2] += fold_lanes(upstream)
            delta = normalize_back(upstream, scaled, spr[:, at], wide(vec[1], BLK)).astype(bf16)
            ehd[64:128, at] = delta
            hidden = mm(w2[...], delta) * slope[:, at]
            sums[0] += fold_lanes(hidden)
            hidden = hidden.astype(bf16)
            ehd[0:64, at] = hidden
            dedges[:, at] = (cotangent + mm(w1[128:192, :], hidden)).astype(bf16)
            return carry

        lax.fori_loop(0, NF // BLK, backward_faces, 0)

        edge_part = mm_last(stk[...], ehd[...])
        node_part = mm_last(nin[...], nh2[...])
        lane64 = lax.broadcasted_iota(jnp.int32, (64, 128), 1)
        vectors = jnp.zeros((64, 128), f32)
        for number in range(6):
            vectors = jnp.where(
                lane64 == 64 + number, jnp.sum(sums[number], axis=1, keepdims=True), vectors
            )
        grads[0:64] = jnp.where(lane64 < 64, edge_part[0:64], node_part[0:64])
        grads[64:128] = jnp.where(lane64 < 64, edge_part[64:128], node_part[64:128])
        grads[128:192] = jnp.where(lane64 < 64, edge_part[128:192], vectors)
        grads[192:256] = jnp.where(lane64 < 64, node_part[128:192], edge_part[192:256])

        first = []
        if comm:
            for j in range(1, 8):
                other, peer = a_peer(j)
                first.append(
                    pltpu.make_async_remote_copy(
                        src_ref=grads.at[pl.ds(pl.multiple_of(other * 32, 32), 32), :],
                        dst_ref=rs_buf.at[a],
                        send_sem=sem_rs.at[j],
                        recv_sem=sem_rr.at[a],
                        device_id=peer,
                        device_id_type=MESH,
                    )
                )
            for copy in first:
                copy.start()

        acc[...] = jnp.zeros_like(acc)

        def sum_ghosts(i, carry):
            at = pl.ds(pl.multiple_of(i * BLK, BLK), BLK)
            lo, hi = col_s[at, 0:128], col_s[at, 128:256]
            part = ehd[0:64, at]
            for tile in range(6):
                where = slice(256 * tile, 256 * tile + 256)
                acc[:, where] += mm(part, selector_t(lo, hi, 4 + tile, iotas))
            return carry

        lax.fori_loop(0, NF // BLK, sum_ghosts, 0)
        for pair in range(NB // 2):
            block = mm(
                w1[0:64, :], acc[:, 256 * pair : 256 * pair + 256].astype(bf16)
            ).astype(bf16)
            gsend[2 * pair] = block[:, :HALO]
            gsend[2 * pair + 1] = block[:, HALO:]
        if comm:
            for number, (o, r) in enumerate(halo_pairs):
                t = lax.rem(s + r, 4)
                backward.append(
                    pltpu.make_async_remote_copy(
                        src_ref=gsend.at[o * 4 + t],
                        dst_ref=gback.at[o * 4 + s],
                        send_sem=sem_bs.at[number],
                        recv_sem=sem_br.at[o * 4 + s],
                        device_id=row_peer(1 - o, r),
                        device_id_type=MESH,
                    )
                )
            for copy in backward:
                copy.start()

        second = []
        if comm:
            total = grads[pl.ds(pl.multiple_of(a * 32, 32), 32), :]
            for j in range(1, 8):
                other, peer = a_peer(j)
                pltpu.make_async_remote_copy(
                    src_ref=rs_buf.at[other],
                    dst_ref=rs_buf.at[other],
                    send_sem=sem_rs.at[j],
                    recv_sem=sem_rr.at[other],
                    device_id=peer,
                    device_id_type=MESH,
                ).wait_recv()
                total = total + rs_buf[other]
            ex_buf[b] = total
            for j in range(1, 16):
                other, peer = b_peer(j)
                second.append(
                    pltpu.make_async_remote_copy(
                        src_ref=ex_buf.at[b],
                        dst_ref=ex_buf.at[b],
                        send_sem=sem_es.at[j],
                        recv_sem=sem_er.at[b],
                        device_id=peer,
                        device_id_type=MESH,
                    )
                )
            for copy in second:
                copy.start()

        acc[:, 0:NC] = jnp.zeros((D, NC), f32)
        gt[...] = jnp.zeros_like(gt)

        def sum_own(i, carry):
            at = pl.ds(pl.multiple_of(i * BLK, BLK), BLK)
            part = ehd[0:64, at]
            for cols, total in ((col_s, acc), (col_r, gt)):
                lo, hi = cols[at, 0:128], cols[at, 128:256]
                for tile in range(4):
                    where = slice(256 * tile, 256 * tile + 256)
                    total[:, where] += mm(part, selector_t(lo, hi, tile, iotas))
            return carry

        lax.fori_loop(0, NF // BLK, sum_own, 0)
        own[...] += mm(w1[0:64, :], acc[:, 0:NC].astype(bf16)) + mm(
            w1[64:128, :], gt[...].astype(bf16)
        )

        third = []
        if comm:
            for j in range(1, 16):
                other, peer = b_peer(j)
                pltpu.make_async_remote_copy(
                    src_ref=ex_buf.at[other],
                    dst_ref=ex_buf.at[other],
                    send_sem=sem_es.at[j],
                    recv_sem=sem_er.at[other],
                    device_id=peer,
                    device_id_type=MESH,
                ).wait_recv()
            total = ex_buf[0]
            for j in range(1, 16):
                total = total + ex_buf[j]
            ag_buf[a] = total
            for j in range(1, 8):
                other, peer = a_peer(j)
                third.append(
                    pltpu.make_async_remote_copy(
                        src_ref=ag_buf.at[a],
                        dst_ref=ag_buf.at[a],
                        send_sem=sem_as.at[j],
                        recv_sem=sem_ar.at[a],
                        device_id=peer,
                        device_id_type=MESH,
                    )
                )
            for copy in third:
                copy.start()

            for o, r in halo_pairs:
                t = lax.rem(s + r, 4)
                pltpu.make_async_remote_copy(
                    src_ref=gsend.at[o * 4 + t],
                    dst_ref=gback.at[o * 4 + t],
                    send_sem=sem_bs.at[0],
                    recv_sem=sem_br.at[o * 4 + t],
                    device_id=row_peer(1 - o, r),
                    device_id_type=MESH,
                ).wait_recv()

        returned = jnp.concatenate([gback[k] for k in range(NB)], axis=1)
        for tile in range(4):
            where = slice(256 * tile, 256 * tile + 256)
            total = own[:, where]
            for pair in range(NB // 2):
                at = slice(256 * pair, 256 * pair + 256)
                total = total + mm(
                    returned[:, at],
                    selector_t(col_p[at, 0:128], col_p[at, 128:256], tile, iotas),
                )
            dstate[:, where] = total.astype(bf16)

        if comm:
            for j in range(1, 8):
                other, peer = a_peer(j)
                pltpu.make_async_remote_copy(
                    src_ref=ag_buf.at[other],
                    dst_ref=ag_buf.at[other],
                    send_sem=sem_as.at[j],
                    recv_sem=sem_ar.at[other],
                    device_id=peer,
                    device_id_type=MESH,
                ).wait_recv()
            whole = jnp.concatenate([ag_buf[j] for j in range(8)], axis=0) * FACTOR
        else:
            whole = grads[...] * FACTOR
        o_w1[...] = whole[0:192, 0:64]
        o_nw2[...] = whole[192:256, 0:64]
        swapped = jnp.concatenate([whole[0:128], whole[192:256]], axis=0)
        swapped = pltpu.roll(swapped, 64, 1)
        o_nw1[...] = swapped[0:128, 0:64]
        o_w2[...] = swapped[128:192, 0:64]
        rows = whole[128:192, :].T
        o_b1[...] = rows[64:65, :]
        o_eg[...] = rows[65:66, :]
        o_es[...] = rows[66:67, :]
        o_nb1[...] = rows[67:68, :]
        o_ng[...] = rows[68:69, :]
        o_ns[...] = rows[69:70, :]
        for copy in forward + backward + first + second + third:
            copy.wait_send()

    return kernel


def call(comm, *args):
    shapes = [
        ((D, NC), bf16),
        ((D, NF), bf16),
        ((192, 64), f32),
        ((1, 64), f32),
        ((64, 64), f32),
        ((1, 64), f32),
        ((1, 64), f32),
        ((128, 64), f32),
        ((1, 64), f32),
        ((64, 64), f32),
        ((1, 64), f32),
        ((1, 64), f32),
    ]
    dma = pltpu.SemaphoreType.DMA
    scratch = [
        pltpu.VMEM((256, NF), bf16),
        pltpu.VMEM((D, NF), f32),
        pltpu.VMEM((D, NF), f32),
        pltpu.VMEM((1, NF), f32),
        pltpu.VMEM((D, NF), bf16),
        pltpu.VMEM((128, NF), bf16),
        pltpu.VMEM((NF, 256), bf16),
        pltpu.VMEM((NF, 256), bf16),
        pltpu.VMEM((NB * HALO, 256), bf16),
        pltpu.VMEM((NB, D, HALO), bf16),
        pltpu.VMEM((NB, D, HALO), bf16),
        pltpu.VMEM((NB, D, HALO), bf16),
        pltpu.VMEM((NB, D, HALO), bf16),
        pltpu.VMEM((192, NC), bf16),
        pltpu.VMEM((128, NC), bf16),
        pltpu.VMEM((D, NC), bf16),
        pltpu.VMEM((D, NC), f32),
        pltpu.VMEM((D, NB * HALO), f32),
        pltpu.VMEM((D, NC), f32),
        pltpu.VMEM((D, HALO), bf16),
        pltpu.VMEM((5, D, 128), f32),
        pltpu.VMEM((6, D, 128), f32),
        pltpu.VMEM((256, 128), f32),
        pltpu.VMEM((8, 32, 128), f32),
        pltpu.VMEM((16, 32, 128), f32),
        pltpu.VMEM((8, 32, 128), f32),
        pltpu.VMEM((64, 192), bf16),
        pltpu.VMEM((64, 64), bf16),
        pltpu.VMEM((64, 128), bf16),
        pltpu.VMEM((64, 64), bf16),
        dma((12,)), dma((12,)), dma((12,)), dma((12,)),
        dma((8,)), dma((8,)), dma((16,)), dma((16,)), dma((8,)), dma((8,)),
    ]
    vmem = pl.BlockSpec(memory_space=pltpu.VMEM)
    params = dict(vmem_limit_bytes=48 * 1024 * 1024)
    if comm:
        params.update(collective_id=0, has_side_effects=True)
    return pl.pallas_call(
        make_kernel(comm),
        out_shape=[jax.ShapeDtypeStruct(shape, kind) for shape, kind in shapes],
        in_specs=[vmem] * 16,
        out_specs=[vmem] * 12,
        scratch_shapes=scratch,
        compiler_params=pltpu.CompilerParams(**params),
        name="layer",
    )(*args)


def on_device(comm, node_state, edge_state, senders, receivers, send_index, node_cotangent, edge_cotangent,
              edge_first, edge_bias, edge_second, edge_gain, edge_shift, node_first, node_bias, node_second, node_gain):
    line = lambda v: v.reshape(1, -1)
    outs = call(
        comm, node_state, edge_state, line(senders), line(receivers), send_index.reshape(NB, HALO),
        node_cotangent, edge_cotangent, edge_first, line(edge_bias), edge_second, line(edge_gain),
        line(edge_shift), node_first, line(node_bias), node_second, line(node_gain),
    )
    return tuple(v.reshape(-1) if v.shape[0] == 1 else v for v in outs)


def solution(mesh):
    split = Mesh(mesh.devices.reshape(4, 4, 2, 4), AXES)
    every = P(None, AXES)
    in_specs = (every, every, P(AXES), P(AXES), P(AXES, None, None), every, every) + (P(),) * 9
    out_specs = (every, every) + (P(),) * 10
    return jax.shard_map(
        lambda *args: on_device(True, *args), mesh=split, in_specs=in_specs, out_specs=out_specs,
        check_vma=False,
    )
```

time: 190 us -> 60.2 us (0.32); the launches traced: 187 us -> 59.7 us
  matrix products: 82.8 us -> 0 us
  starting transfers between devices: 48.7 us -> 0 us
  Pallas kernels: 0 us -> 43.1 us
  waiting for transfers between devices: 14.4 us -> 0 us
  other arithmetic: 10.9 us -> 0 us
  local copies, waits for them, and re-layouts: 26.8 us -> 15.9 us
    dot_general x102 -> x0, matrix products: 82.8 us -> none  [the longest x45 55.1 us: one_block(): jnp.dot(portion, selector, precision=precision, preferred_element_type=jn...]
    pallas_call x0 -> x1, Pallas kernels: none -> 43.1 us  [call(): pl.pallas_call(make_kernel(comm), out_shape=[jax.ShapeDtypeStruct(shape,...]
    all_to_all x6 -> x0, starting transfers between devices: 36.4 us -> none  [the longest x2 14 us: copy_for_each(): lax.all_to_all(jnp.broadcast_to(array[None], (peers, *array.shape)), axis...]
    all_to_all x6 -> x0, waiting for transfers between devices: 13.9 us -> none  [the longest x2 5.54 us: copy_for_each(): lax.all_to_all(jnp.broadcast_to(array[None], (peers, *array.shape)), axis...]
    ppermute x4 -> x0, starting transfers between devices: 12.3 us -> none  [from_behind(): lax.ppermute(value, axis, [(source, source + steps) for source in range(f...]
    unnamed x61 -> x41, local copies, waits for them, and re-layouts: 3.91 us -> 15.9 us
    dynamic_slice x42 -> x0, local copies, waits for them, and re-layouts: 6.82 us -> none  [one_block(): chosen = lax.dynamic_index_in_dim(blocks, number, 0, keepdims=False)]
    reshape x10 -> x0, local copies, waits for them, and re-layouts: 5.41 us -> none  [the longest x4 5.11 us: packed_total(): running = total_of(jnp.concatenate([a.ravel() for a in arrays]), axis)]
  transfers between devices with their start and end apart: 10 -> 0, of which waited for: 4 -> 0; matrix products, arithmetic and copies ran while one was open for 37% -> 0% of each run, Pallas kernels for 0% -> 0%
where the time goes in v1:
time: 60.2 us; the launch traced here: 59.7 us
  Pallas kernels  43.1 us (72%)
  local copies, waits for them, and re-layouts  15.9 us (26%)
  between operations  0.76 us (1%)
    pallas_call x1, Pallas kernels, call(): pl.pallas_call(make_kernel(comm), out_shape=[jax.ShapeDtypeStruct(shape,...  43.1 us
    unnamed x41, local copies, waits for them, and re-layouts  15.9 us

profile of v1, /device:TPU:1, one launch (start us, length us, event | category | flops | bytes accessed | tf_op | source)
XLA Modules:
  0.0 59.7 jit_solution(5357144854087104435)
XLA Ops:
  0.7 0.7 %copy.34 = s32[1,12,128]{2,1,0:T(8,128)S(1)} copy(s32[1,12,128]{2,0,1:T(1,128)} %param.20) | data formatting | bytes 12288
  1.4 0.8 %copy.29.nw1 = bf16[128,64]{1,0:T(8,128)(2,1)S(1)} copy(bf16[128,64]{0,1:T(8,128)(2,1)} %param.28) | data formatting | bytes 32768 | tf_op args[12]
  2.2 0.0 copy-start.4
  2.2 0.0 copy-start.6
  2.2 0.0 copy-start.8
  2.2 0.0 copy-start.9
  2.3 0.9 %copy.28.w1 = bf16[192,64]{1,0:T(8,128)(2,1)S(1)} copy(bf16[192,64]{0,1:T(8,128)(2,1)} %param.23) | data formatting | bytes 49152 | tf_op args[7]
  3.1 0.0 copy-done.2
  3.2 0.0 copy-done.4
  3.2 0.0 copy-done.6
  3.2 0.0 copy-start
  3.2 1.0 %copy-done = bf16[64,3072]{1,0:T(8,128)(2,1)S(1)} copy-done((bf16[64,3072]{1,0:T(8,128)(2,1)S(1)}, bf16[64,3072]{1,0:T(8,128)(2,1)}, u32[]{:S(2)}) %copy-start) | copy-done | bytes 393240
  4.2 1.0 %copy-done.1 = bf16[64,3072]{1,0:T(8,128)(2,1)S(1)} copy-done((bf16[64,3072]{1,0:T(8,128)(2,1)S(1)}, bf16[64,3072]{1,0:T(8,128)(2,1)}, u32[]{:S(2)}) %copy-start.1) | copy-done | bytes 393240
  5.2 0.9 %copy-done.3 = bf16[64,1024]{1,0:T(8,128)(2,1)S(1)} copy-done((bf16[64,1024]{1,0:T(8,128)(2,1)S(1)}, bf16[64,1024]{1,0:T(8,128)(2,1)}, u32[]{:S(2)}) %copy-start.3) | copy-done | bytes 131096
  6.1 0.7 %copy-done.5 = bf16[64,64]{1,0:T(8,128)(2,1)S(1)} copy-done((bf16[64,64]{1,0:T(8,128)(2,1)S(1)}, bf16[64,64]{1,0:T(8,128)(2,1)}, u32[]{:S(2)}) %copy-start.5) | copy-done | bytes 8216
  6.8 0.7 %copy-done.7 = s32[3072]{0:T(1024)S(1)} copy-done((s32[3072]{0:T(1024)S(1)}, s32[3072]{0:T(1024)}, u32[]{:S(2)}) %copy-start.7) | copy-done | bytes 12312
  7.5 0.7 %copy-done.10 = f32[64]{0:T(128)S(1)} copy-done((f32[64]{0:T(128)S(1)}, f32[64]{0:T(128)}, u32[]{:S(2)}) %copy-start.10) | copy-done | bytes 280
  8.2 0.7 %copy-done.11 = f32[64]{0:T(128)S(1)} copy-done((f32[64]{0:T(128)S(1)}, f32[64]{0:T(128)}, u32[]{:S(2)}) %copy-start.11) | copy-done | bytes 280
  8.8 0.7 %copy-done.12 = f32[64]{0:T(128)S(1)} copy-done((f32[64]{0:T(128)S(1)}, f32[64]{0:T(128)}, u32[]{:S(2)}) %copy-start.12) | copy-done | bytes 280
  9.5 43.1 %layer.1 = (bf16[64,1024]{1,0:T(8,128)(2,1)S(1)}, bf16[64,3072]{1,0:T(8,128)(2,1)S(1)}, f32[192,64]{1,0:T(8,128)S(1)}, f32[1,64]{1,0:T(1,128)S(1)}, f32[64,64]{1...) custom-call(bf16[64,1024]{1,0:T(8,128)(2,1)S(1)} %copy-done.2, ...), custom_call_target="tpu_custom_call" | custom-call | tf_op jit(solution)/shard_map/layer/pallas_call | solution.py:565
  52.6 0.7 %copy.31 = f32[128,64]{0,1:T(8,128)} copy(f32[128,64]{1,0:T(8,128)S(1)} %get-tuple-element.43) | data formatting | bytes 65536
  53.3 0.7 %copy.30 = f32[192,64]{0,1:T(8,128)} copy(f32[192,64]{1,0:T(8,128)S(1)} %get-tuple-element.38) | data formatting | bytes 98304
  54.0 0.7 %copy.45 = bf16[64,1024]{1,0:T(8,128)(2,1)} copy(bf16[64,1024]{1,0:T(8,128)(2,1)S(1)} %get-tuple-element.60) | data formatting | bytes 262144
  54.7 0.7 %copy.46 = bf16[64,3072]{1,0:T(8,128)(2,1)} copy(bf16[64,3072]{1,0:T(8,128)(2,1)S(1)} %get-tuple-element.61) | data formatting | bytes 786432
  55.4 0.5 copy.47
  55.9 0.6 %copy.48 = f32[64,64]{1,0:T(8,128)} copy(f32[64,64]{1,0:T(8,128)S(1)} %get-tuple-element.64) | data formatting | bytes 32768
  56.5 0.5 copy.49
  57.0 0.5 copy.50
  57.6 0.5 copy.51
  58.1 0.6 %copy.52 = f32[64,64]{1,0:T(8,128)} copy(f32[64,64]{1,0:T(8,128)S(1)} %get-tuple-element.69) | data formatting | bytes 32768
  58.7 0.5 copy.53
  59.2 0.5 copy.54
  (10 shorter events, 0.0 us)
Async XLA Ops:
  0.6 2.5 %copy-start.2 = (bf16[64,1024]{1,0:T(8,128)(2,1)S(1)}, bf16[64,1024]{1,0:T(8,128)(2,1)}, u32[]{:S(2)}) copy-start(bf16[64,1024]{1,0:T(8,128)(2,1)} %ns.1) | copy-start | bytes 393220
  2.2 1.0 %copy-start.4 = (bf16[64,64]{1,0:T(8,128)(2,1)S(1)}, bf16[64,64]{1,0:T(8,128)(2,1)}, u32[]{:S(2)}) copy-start(bf16[64,64]{1,0:T(8,128)(2,1)} %w2.1) | copy-start | bytes 24580
  2.2 0.9 %copy-start.6 = (s32[3072]{0:T(1024)S(1)}, s32[3072]{0:T(1024)}, u32[]{:S(2)}) copy-start(s32[3072]{0:T(1024)} %param.18) | copy-start | bytes 36868
  2.2 0.9 %copy-start.8 = (f32[64]{0:T(128)S(1)}, f32[64]{0:T(128)}, u32[]{:S(2)}) copy-start(f32[64]{0:T(128)} %param.24) | copy-start | bytes 772
  2.2 0.9 %copy-start.9 = (f32[64]{0:T(128)S(1)}, f32[64]{0:T(128)}, u32[]{:S(2)}) copy-start(f32[64]{0:T(128)} %param.26) | copy-start | bytes 772
  3.2 1.0 %copy-start = (bf16[64,3072]{1,0:T(8,128)(2,1)S(1)}, bf16[64,3072]{1,0:T(8,128)(2,1)}, u32[]{:S(2)}) copy-start(bf16[64,3072]{1,0:T(8,128)(2,1)} %es.1) | copy-start | bytes 1179652
  4.2 1.0 %copy-start.1 = (bf16[64,3072]{1,0:T(8,128)(2,1)S(1)}, bf16[64,3072]{1,0:T(8,128)(2,1)}, u32[]{:S(2)}) copy-start(bf16[64,3072]{1,0:T(8,128)(2,1)} %ect.1) | copy-start | bytes 1179652
  5.2 0.9 %copy-start.3 = (bf16[64,1024]{1,0:T(8,128)(2,1)S(1)}, bf16[64,1024]{1,0:T(8,128)(2,1)}, u32[]{:S(2)}) copy-start(bf16[64,1024]{1,0:T(8,128)(2,1)} %nct.1) | copy-start | bytes 393220
  6.1 0.7 %copy-start.5 = (bf16[64,64]{1,0:T(8,128)(2,1)S(1)}, bf16[64,64]{1,0:T(8,128)(2,1)}, u32[]{:S(2)}) copy-start(bf16[64,64]{1,0:T(8,128)(2,1)} %nw2.1) | copy-start | bytes 24580
  6.8 0.7 %copy-start.7 = (s32[3072]{0:T(1024)S(1)}, s32[3072]{0:T(1024)}, u32[]{:S(2)}) copy-start(s32[3072]{0:T(1024)} %param.19) | copy-start | bytes 36868
  7.5 0.7 %copy-start.10 = (f32[64]{0:T(128)S(1)}, f32[64]{0:T(128)}, u32[]{:S(2)}) copy-start(f32[64]{0:T(128)} %param.27) | copy-start | bytes 772
  8.2 0.7 %copy-start.11 = (f32[64]{0:T(128)S(1)}, f32[64]{0:T(128)}, u32[]{:S(2)}) copy-start(f32[64]{0:T(128)} %param.29) | copy-start | bytes 772
  8.8 0.7 %copy-start.12 = (f32[64]{0:T(128)S(1)}, f32[64]{0:T(128)}, u32[]{:S(2)}) copy-start(f32[64]{0:T(128)} %param.31) | copy-start | bytes 772

commit v2 on v1

--- a/solution.py
+++ b/solution.py
@@ -107,13 +107,24 @@
 
 def make_kernel(comm):
     def kernel(
-        ns, es, snd, rcv, six, nct, ect, w1, b1, w2, eg, esh, nw1, nb1, nw2, ng,
-        dstate, dedges, o_w1, o_b1, o_w2, o_eg, o_es, o_nw1, o_nb1, o_nw2, o_ng, o_ns,
-        stk, slope, scl, spr, msg, ehd, col_s, col_r, col_p,
-        sendb, ghost, gsend, gback, nin, nh2, nbr, own, acc, gt, gsb,
-        vec, sums, grads, rs_buf, ex_buf, ag_buf, w1t, w2t, nw1t, nw2t,
-        sem_fs, sem_fr, sem_bs, sem_br, sem_rs, sem_rr, sem_es, sem_er, sem_as, sem_ar,
+        *refs
     ):
+        given, refs = refs[:16], refs[16:]
+        (dstate, dedges, packed), refs = refs[:3], refs[3:]
+        held, refs = refs[:16], refs[16:]
+        (
+            stk, slope, scl, spr, msg, ehd, col_s, col_r, col_p,
+            sendb, ghost, gsend, gback, nin, nh2, nbr, own, acc, gt, gsb,
+            vec, sums, grads, rs_buf, ex_buf, ag_buf, w1, w2t, nw1, nw2t,
+            sem_fs, sem_fr, sem_bs, sem_br, sem_rs, sem_rr, sem_es, sem_er, sem_as, sem_ar,
+            sem_in,
+        ) = refs
+        ns, es, snd, rcv, six, nct, ect, w1t, b1, w2, eg, esh, nw1t, nb1, nw2, ng = held
+        loads = [
+            pltpu.make_async_copy(given[k], held[k], sem_in.at[k]) for k in range(16)
+        ]
+        for k in (4, 0, 2, 3, 1, 7, 8, 9, 10, 11, 12, 13, 14, 15, 5, 6):
+            loads[k].start()
         if comm:
             z = lax.axis_index("z")
             y = lax.axis_index("y")
@@ -153,8 +164,10 @@
         iota2 = jnp.concatenate([iota, iota], axis=1)
         iotas = lane_iotas()
 
+        loads[4].wait()
+        loads[0].wait()
         for pair in range(NB // 2):
-            row = jnp.concatenate([six[2 * pair : 2 * pair + 1, :], six[2 * pair + 1 : 2 * pair + 2, :]], axis=1)
+            row = six[:, 256 * pair : 256 * pair + 256]
             lo, hi = split_index(row)
             picked = jnp.zeros((D, 256), f32)
             for tile in range(4):
@@ -188,14 +201,16 @@
             for copy in forward:
                 copy.start()
 
+        for k in (2, 3, 1, 7, 8, 9, 10, 11, 12, 13, 14, 15):
+            loads[k].wait()
         vec[0] = column_of(b1[...])
         vec[1] = column_of(eg[...])
         vec[2] = column_of(esh[...])
         vec[3] = column_of(nb1[...])
         vec[4] = column_of(ng[...])
-        w1t[...] = w1[...].astype(f32).T.astype(bf16)
+        w1[...] = w1t[...].astype(f32).T.astype(bf16)
         w2t[...] = w2[...].astype(f32).T.astype(bf16)
-        nw1t[...] = nw1[...].astype(f32).T.astype(bf16)
+        nw1[...] = nw1t[...].astype(f32).T.astype(bf16)
         nw2t[...] = nw2[...].astype(f32).T.astype(bf16)
         sums[...] = jnp.zeros_like(sums)
         stk[128:192, :] = es[...]
@@ -262,6 +277,8 @@
 
         lax.fori_loop(0, NF // BLK, sum_messages, 0)
 
+        loads[5].wait()
+        loads[6].wait()
         def cells(i, carry):
             at = pl.ds(pl.multiple_of(i * BLK, BLK), BLK)
             nin[64:128, at] = acc[:, at].astype(bf16)
@@ -486,45 +503,63 @@
                     device_id=peer,
                     device_id_type=MESH,
                 ).wait_recv()
-            whole = jnp.concatenate([ag_buf[j] for j in range(8)], axis=0) * FACTOR
+            for j in range(8):
+                packed[32 * j : 32 * j + 32] = ag_buf[j]
         else:
-            whole = grads[...] * FACTOR
-        o_w1[...] = whole[0:192, 0:64]
-        o_nw2[...] = whole[192:256, 0:64]
-        swapped = jnp.concatenate([whole[0:128], whole[192:256]], axis=0)
-        swapped = pltpu.roll(swapped, 64, 1)
-        o_nw1[...] = swapped[0:128, 0:64]
-        o_w2[...] = swapped[128:192, 0:64]
-        rows = whole[128:192, :].T
-        o_b1[...] = rows[64:65, :]
-        o_eg[...] = rows[65:66, :]
-        o_es[...] = rows[66:67, :]
-        o_nb1[...] = rows[67:68, :]
-        o_ng[...] = rows[68:69, :]
-        o_ns[...] = rows[69:70, :]
+            packed[...] = grads[...]
         for copy in forward + backward + first + second + third:
             copy.wait_send()
 
     return kernel
+
+
+def finish(
+    dstate, dedges, packed, out_state, out_edges, *refs
+):
+    results, refs = refs[:10], refs[10:]
+    staged, sems = refs[:10], refs[10]
+    o_w1, o_b1, o_w2, o_eg, o_es, o_nw1, o_nb1, o_nw2, o_ng, o_ns = staged
+    stores = [
+        pltpu.make_async_copy(dedges, out_edges, sems.at[10]),
+        pltpu.make_async_copy(dstate, out_state, sems.at[11]),
+    ]
+    for copy in stores:
+        copy.start()
+    whole = packed[...] * FACTOR
+    turned = jnp.concatenate([whole[0:128].T, whole[128:256].T], axis=1)
+    o_w1[...] = turned[0:64, 0:192]
+    o_nw1[...] = turned[64:128, 0:128]
+    o_nw2[...] = whole[192:256, 0:64]
+    o_w2[...] = pltpu.roll(whole[192:256], 64, 1)[:, 0:64]
+    rows = turned[64:128, 128:192]
+    for k, ref in enumerate((o_b1, o_eg, o_es, o_nb1, o_ng, o_ns)):
+        ref[...] = rows[k : k + 1, :]
+    for k in range(10):
+        copy = pltpu.make_async_copy(staged[k], results[k], sems.at[k])
+        copy.start()
+        stores.append(copy)
+    for copy in stores:
+        copy.wait()
 
 
 def call(comm, *args):
     shapes = [
         ((D, NC), bf16),
         ((D, NF), bf16),
-        ((192, 64), f32),
+        ((64, 192), f32),
         ((1, 64), f32),
         ((64, 64), f32),
         ((1, 64), f32),
         ((1, 64), f32),
-        ((128, 64), f32),
+        ((64, 128), f32),
         ((1, 64), f32),
         ((64, 64), f32),
         ((1, 64), f32),
         ((1, 64), f32),
     ]
     dma = pltpu.SemaphoreType.DMA
-    scratch = [
+    scratch = [pltpu.VMEM(arg.shape, arg.dtype) for arg in args]
+    scratch += [
         pltpu.VMEM((256, NF), bf16),
         pltpu.VMEM((D, NF), f32),
         pltpu.VMEM((D, NF), f32),
@@ -551,37 +586,53 @@
         pltpu.VMEM((8, 32, 128), f32),
         pltpu.VMEM((16, 32, 128), f32),
         pltpu.VMEM((8, 32, 128), f32),
-        pltpu.VMEM((64, 192), bf16),
+        pltpu.VMEM((192, 64), bf16),
         pltpu.VMEM((64, 64), bf16),
-        pltpu.VMEM((64, 128), bf16),
+        pltpu.VMEM((128, 64), bf16),
         pltpu.VMEM((64, 64), bf16),
         dma((12,)), dma((12,)), dma((12,)), dma((12,)),
         dma((8,)), dma((8,)), dma((16,)), dma((16,)), dma((8,)), dma((8,)),
+        dma((16,)),
     ]
-    vmem = pl.BlockSpec(memory_space=pltpu.VMEM)
-    params = dict(vmem_limit_bytes=48 * 1024 * 1024)
+    anywhere = pl.BlockSpec(memory_space=pltpu.HBM)
+    params = dict(vmem_limit_bytes=36 * 1024 * 1024)
     if comm:
         params.update(collective_id=0, has_side_effects=True)
-    return pl.pallas_call(
+    vmem = pl.BlockSpec(memory_space=pltpu.VMEM)
+    middle = pl.pallas_call(
         make_kernel(comm),
-        out_shape=[jax.ShapeDtypeStruct(shape, kind) for shape, kind in shapes],
-        in_specs=[vmem] * 16,
-        out_specs=[vmem] * 12,
+        out_shape=[
+            jax.ShapeDtypeStruct(shape, kind) for shape, kind in shapes[:2] + [((256, 128), f32)]
+        ],
+        in_specs=[anywhere] * 16,
+        out_specs=[vmem] * 3,
         scratch_shapes=scratch,
         compiler_params=pltpu.CompilerParams(**params),
         name="layer",
     )(*args)
+    return pl.pallas_call(
+        finish,
+        out_shape=[jax.ShapeDtypeStruct(shape, kind) for shape, kind in shapes],
+        in_specs=[vmem] * 3,
+        out_specs=[anywhere] * 12,
+        scratch_shapes=[pltpu.VMEM(shape, kind) for shape, kind in shapes[2:]] + [dma((12,))],
+        compiler_params=pltpu.CompilerParams(vmem_limit_bytes=8 * 1024 * 1024),
+        name="finish",
+    )(*middle)
 
 
 def on_device(comm, node_state, edge_state, senders, receivers, send_index, node_cotangent, edge_cotangent,
               edge_first, edge_bias, edge_second, edge_gain, edge_shift, node_first, node_bias, node_second, node_gain):
     line = lambda v: v.reshape(1, -1)
     outs = call(
-        comm, node_state, edge_state, line(senders), line(receivers), send_index.reshape(NB, HALO),
-        node_cotangent, edge_cotangent, edge_first, line(edge_bias), edge_second, line(edge_gain),
-        line(edge_shift), node_first, line(node_bias), node_second, line(node_gain),
+        comm, node_state, edge_state, line(senders), line(receivers), line(send_index),
+        node_cotangent, edge_cotangent, edge_first.T, line(edge_bias), edge_second, line(edge_gain),
+        line(edge_shift), node_first.T, line(node_bias), node_second, line(node_gain),
     )
-    return tuple(v.reshape(-1) if v.shape[0] == 1 else v for v in outs)
+    outs = [v.reshape(-1) if v.shape[0] == 1 else v for v in outs]
+    outs[2] = outs[2].T
+    outs[7] = outs[7].T
+    return tuple(outs)
 
 
 def solution(mesh):

time: 60.2 us -> 55.3 us (0.919)
  local copies, waits for them, and re-layouts: 15.9 us -> 8.77 us
  Pallas kernels: 43.1 us -> 45.2 us
    unnamed x41 -> x32, local copies, waits for them, and re-layouts: 15.9 us -> 8.77 us
    pallas_call x1, Pallas kernels: 43.1 us -> 44.2 us  [call(): pl.pallas_call(make_kernel(comm), out_shape=[jax.ShapeDtypeStruct(shape,...]
    pallas_call x0 -> x1, Pallas kernels: none -> 0.96 us  [call(): pl.pallas_call(finish, out_shape=[jax.ShapeDtypeStruct(shape, kind) for s...]
where the time goes in v2:
time: 55.3 us; the launch traced here: 54.7 us
  Pallas kernels  45.2 us (82%)
  local copies, waits for them, and re-layouts  8.77 us (16%)
  between operations  0.73 us (1%)
    pallas_call x1, Pallas kernels, call(): pl.pallas_call(make_kernel(comm), out_shape=[jax.ShapeDtypeStruct(shape,...  44.2 us
    unnamed x32, local copies, waits for them, and re-layouts  8.77 us

profile of v2, /device:TPU:1, one launch (start us, length us, event | category | flops | bytes accessed | tf_op | source)
XLA Modules:
  0.0 54.7 jit_solution(8798288822971255501)
XLA Ops:
  0.7 0.0 copy-start.5
  0.7 0.0 copy-start.14
  0.7 0.0 copy-start.15
  0.7 0.0 copy-start.11
  0.7 0.0 copy-start.12
  0.7 0.0 copy-start.13
  0.7 0.7 %copy-done.5 = bf16[64,64]{1,0:T(8,128)(2,1)S(1)} copy-done((bf16[64,64]{1,0:T(8,128)(2,1)S(1)}, bf16[64,64]{1,0:T(8,128)(2,1)}, u32[]{:S(2)}) %copy-start.5) | copy-done | bytes 8216
  1.4 0.0 copy-done.14
  1.4 0.0 copy-done.15
  1.4 0.0 copy-done.11
  1.4 0.0 copy-done.12
  1.4 0.0 copy-done.13
  1.4 0.0 copy-start
  1.4 1.0 %copy-done = bf16[64,3072]{1,0:T(8,128)(2,1)S(1)} copy-done((bf16[64,3072]{1,0:T(8,128)(2,1)S(1)}, bf16[64,3072]{1,0:T(8,128)(2,1)}, u32[]{:S(2)}) %copy-start) | copy-done | bytes 393240
  2.4 0.0 copy-start.1
  2.4 1.0 %copy-done.1 = bf16[64,3072]{1,0:T(8,128)(2,1)S(1)} copy-done((bf16[64,3072]{1,0:T(8,128)(2,1)S(1)}, bf16[64,3072]{1,0:T(8,128)(2,1)}, u32[]{:S(2)}) %copy-start.1) | copy-done | bytes 393240
  3.4 0.0 copy-start.2
  3.4 0.9 %copy-done.2 = bf16[64,1024]{1,0:T(8,128)(2,1)S(1)} copy-done((bf16[64,1024]{1,0:T(8,128)(2,1)S(1)}, bf16[64,1024]{1,0:T(8,128)(2,1)}, u32[]{:S(2)}) %copy-start.2) | copy-done | bytes 131096
  4.3 0.0 copy-start.3
  4.3 0.9 %copy-done.3 = bf16[64,1024]{1,0:T(8,128)(2,1)S(1)} copy-done((bf16[64,1024]{1,0:T(8,128)(2,1)S(1)}, bf16[64,1024]{1,0:T(8,128)(2,1)}, u32[]{:S(2)}) %copy-start.3) | copy-done | bytes 131096
  5.2 0.0 copy-start.4
  5.2 0.8 %copy-done.4 = bf16[192,64]{0,1:T(8,128)(2,1)S(1)} copy-done((bf16[192,64]{0,1:T(8,128)(2,1)S(1)}, bf16[192,64]{0,1:T(8,128)(2,1)}, u32[]{:S(2)}) %copy-start.4) | copy-done | bytes 24600
  6.0 0.0 copy-start.6
  6.0 0.7 %copy-done.6 = bf16[128,64]{0,1:T(8,128)(2,1)S(1)} copy-done((bf16[128,64]{0,1:T(8,128)(2,1)S(1)}, bf16[128,64]{0,1:T(8,128)(2,1)}, u32[]{:S(2)}) %copy-start.6) | copy-done | bytes 16408
  6.7 0.0 copy-start.7
  6.7 0.7 %copy-done.7 = bf16[64,64]{1,0:T(8,128)(2,1)S(1)} copy-done((bf16[64,64]{1,0:T(8,128)(2,1)S(1)}, bf16[64,64]{1,0:T(8,128)(2,1)}, u32[]{:S(2)}) %copy-start.7) | copy-done | bytes 8216
  7.4 0.0 copy-start.8
  7.4 0.7 %copy-done.8 = s32[3072]{0:T(1024)S(1)} copy-done((s32[3072]{0:T(1024)S(1)}, s32[3072]{0:T(1024)}, u32[]{:S(2)}) %copy-start.8) | copy-done | bytes 12312
  8.1 0.7 %copy-done.9 = s32[3072]{0:T(1024)S(1)} copy-done((s32[3072]{0:T(1024)S(1)}, s32[3072]{0:T(1024)}, u32[]{:S(2)}) %copy-start.9) | copy-done | bytes 12312
  8.8 0.7 %copy-done.10 = s32[1,12,128]{2,0,1:T(1,128)S(1)} copy-done((s32[1,12,128]{2,0,1:T(1,128)S(1)}, s32[1,12,128]{2,0,1:T(1,128)}, u32[]{:S(2)}) %copy-start.10) | copy-done | bytes 6168
  9.5 44.2 %layer.1 = (bf16[64,1024]{1,0:T(8,128)(2,1)S(1)}, bf16[64,3072]{1,0:T(8,128)(2,1)S(1)}, f32[256,128]{1,0:T(8,128)S(1)}) custom-call(bf16[64,1024]{1,0:T(8,128)(2,1)S(1)} %copy-done.2, bf16[64,3072]{1,0:T(8,128)(2,1)S(1)} %copy-done, s32[1,3072]{1,0:T(1,128)S(1)} %bitcast.20, s32[1,3072]{1,0:T(1,128)S(1)} %bitcast.21, s32[1,1536]{1,0:T(1,128)S(1)} %bitcast.22, ...), custom_call_target="tpu_custom_call" | custom-call | tf_op jit(solution)/shard_map/layer/pallas_call | solution.py:602
  53.7 1.0 %finish.1 = (bf16[64,1024]{1,0:T(8,128)(2,1)}, bf16[64,3072]{1,0:T(8,128)(2,1)}, f32[64,192]{1,0:T(8,128)}, f32[1,64]{1,0:T(1,128)}, f32[64,64]{1,0:T(8,128)}, /...) custom-call(bf16[64,1024]{1,0:T(8,128)(2,1)S(1)} %get-tuple-element., ...), custom_call_target="tpu_custom_call" | custom-call | tf_op jit(solution)/shard_map/finish/pallas_call | solution.py:613
  (2 shorter events, 0.0 us)
Async XLA Ops:
  0.7 0.7 %copy-start.5 = (bf16[64,64]{1,0:T(8,128)(2,1)S(1)}, bf16[64,64]{1,0:T(8,128)(2,1)}, u32[]{:S(2)}) copy-start(bf16[64,64]{1,0:T(8,128)(2,1)} %refs_9_.1) | copy-start | bytes 24580
  0.7 0.7 %copy-start.14 = (f32[64]{0:T(128)S(1)}, f32[64]{0:T(128)}, u32[]{:S(2)}) copy-start(f32[64]{0:T(128)} %param.29) | copy-start | bytes 772
  0.7 0.7 %copy-start.15 = (f32[64]{0:T(128)S(1)}, f32[64]{0:T(128)}, u32[]{:S(2)}) copy-start(f32[64]{0:T(128)} %param.31) | copy-start | bytes 772
  0.7 0.7 %copy-start.11 = (f32[64]{0:T(128)S(1)}, f32[64]{0:T(128)}, u32[]{:S(2)}) copy-start(f32[64]{0:T(128)} %param.24) | copy-start | bytes 772
  0.7 0.7 %copy-start.12 = (f32[64]{0:T(128)S(1)}, f32[64]{0:T(128)}, u32[]{:S(2)}) copy-start(f32[64]{0:T(128)} %param.26) | copy-start | bytes 772
  0.7 0.7 %copy-start.13 = (f32[64]{0:T(128)S(1)}, f32[64]{0:T(128)}, u32[]{:S(2)}) copy-start(f32[64]{0:T(128)} %param.27) | copy-start | bytes 772
  1.4 1.0 %copy-start = (bf16[64,3072]{1,0:T(8,128)(2,1)S(1)}, bf16[64,3072]{1,0:T(8,128)(2,1)}, u32[]{:S(2)}) copy-start(bf16[64,3072]{1,0:T(8,128)(2,1)} %refs_1_.1) | copy-start | bytes 1179652
  2.4 1.0 %copy-start.1 = (bf16[64,3072]{1,0:T(8,128)(2,1)S(1)}, bf16[64,3072]{1,0:T(8,128)(2,1)}, u32[]{:S(2)}) copy-start(bf16[64,3072]{1,0:T(8,128)(2,1)} %refs_6_.1) | copy-start | bytes 1179652
  3.4 0.9 %copy-start.2 = (bf16[64,1024]{1,0:T(8,128)(2,1)S(1)}, bf16[64,1024]{1,0:T(8,128)(2,1)}, u32[]{:S(2)}) copy-start(bf16[64,1024]{1,0:T(8,128)(2,1)} %refs_0_.1) | copy-start | bytes 393220
  4.3 0.9 %copy-start.3 = (bf16[64,1024]{1,0:T(8,128)(2,1)S(1)}, bf16[64,1024]{1,0:T(8,128)(2,1)}, u32[]{:S(2)}) copy-start(bf16[64,1024]{1,0:T(8,128)(2,1)} %refs_5_.1) | copy-start | bytes 393220
  5.2 0.8 %copy-start.4 = (bf16[192,64]{0,1:T(8,128)(2,1)S(1)}, bf16[192,64]{0,1:T(8,128)(2,1)}, u32[]{:S(2)}) copy-start(bf16[192,64]{0,1:T(8,128)(2,1)} %param.23) | copy-start | bytes 73732
  6.0 0.7 %copy-start.6 = (bf16[128,64]{0,1:T(8,128)(2,1)S(1)}, bf16[128,64]{0,1:T(8,128)(2,1)}, u32[]{:S(2)}) copy-start(bf16[128,64]{0,1:T(8,128)(2,1)} %param.28) | copy-start | bytes 49156
  6.7 0.7 %copy-start.7 = (bf16[64,64]{1,0:T(8,128)(2,1)S(1)}, bf16[64,64]{1,0:T(8,128)(2,1)}, u32[]{:S(2)}) copy-start(bf16[64,64]{1,0:T(8,128)(2,1)} %refs_14_.1) | copy-start | bytes 24580
  7.4 0.7 %copy-start.8 = (s32[3072]{0:T(1024)S(1)}, s32[3072]{0:T(1024)}, u32[]{:S(2)}) copy-start(s32[3072]{0:T(1024)} %param.18) | copy-start | bytes 36868
  8.1 0.7 %copy-start.9 = (s32[3072]{0:T(1024)S(1)}, s32[3072]{0:T(1024)}, u32[]{:S(2)}) copy-start(s32[3072]{0:T(1024)} %param.19) | copy-start | bytes 36868
  8.8 0.7 %copy-start.10 = (s32[1,12,128]{2,0,1:T(1,128)S(1)}, s32[1,12,128]{2,0,1:T(1,128)}, u32[]{:S(2)}) copy-start(s32[1,12,128]{2,0,1:T(1,128)} %param.20) | copy-start | bytes 18436

commit v3 on v2

--- a/solution.py
+++ b/solution.py
@@ -217,7 +217,7 @@
         nin[0:64, :] = ns[...]
 
         def gather_own(i, carry):
-            at = pl.ds(pl.multiple_of(i * BLK, BLK), BLK)
+            at = pl.ds(pl.multiple_of(i * BLK, BLK), BLK) if not isinstance(i, int) else slice(i * BLK, i * BLK + BLK)
             for index, begin, cols in ((snd, 0, col_s), (rcv, 64, col_r)):
                 lo, hi = split_index(index[:, at])
                 total = jnp.zeros((D, BLK), f32)
@@ -229,7 +229,8 @@
                 cols[at, :] = columns_of(lo, hi)
             return carry
 
-        lax.fori_loop(0, NF // BLK, gather_own, 0)
+        for i in range(NF // BLK):
+            gather_own(i, 0)
 
         if comm:
             for o, r in halo_pairs:
@@ -244,7 +245,7 @@
                 ).wait_recv()
 
         def forward_faces(i, carry):
-            at = pl.ds(pl.multiple_of(i * BLK, BLK), BLK)
+            at = pl.ds(pl.multiple_of(i * BLK, BLK), BLK) if not isinstance(i, int) else slice(i * BLK, i * BLK + BLK)
             lo, hi = split_index(snd[:, at])
             total = stk[0:64, at].astype(f32)
             for pair in range(NB // 2):
@@ -262,12 +263,13 @@
             msg[:, at] = (scaled * wide(vec[1], BLK) + wide(vec[2], BLK)).astype(bf16)
             return carry
 
-        lax.fori_loop(0, NF // BLK, forward_faces, 0)
+        for i in range(NF // BLK):
+            forward_faces(i, 0)
 
         acc[:, 0:NC] = jnp.zeros((D, NC), f32)
 
         def sum_messages(i, carry):
-            at = pl.ds(pl.multiple_of(i * BLK, BLK), BLK)
+            at = pl.ds(pl.multiple_of(i * BLK, BLK), BLK) if not isinstance(i, int) else slice(i * BLK, i * BLK + BLK)
             lo, hi = col_r[at, 0:128], col_r[at, 128:256]
             part = msg[:, at]
             for tile in range(4):
@@ -275,12 +277,13 @@
                 acc[:, where] += mm(part, selector_t(lo, hi, tile, iotas))
             return carry
 
-        lax.fori_loop(0, NF // BLK, sum_messages, 0)
+        for i in range(NF // BLK):
+            sum_messages(i, 0)
 
         loads[5].wait()
         loads[6].wait()
         def cells(i, carry):
-            at = pl.ds(pl.multiple_of(i * BLK, BLK), BLK)
+            at = pl.ds(pl.multiple_of(i * BLK, BLK), BLK) if not isinstance(i, int) else slice(i * BLK, i * BLK + BLK)
             nin[64:128, at] = acc[:, at].astype(bf16)
             linear = mm(nw1t[...], nin[0:128, at]) + wide(vec[3], BLK)
             gate = logistic(linear)
@@ -301,10 +304,11 @@
             nbr[:, at] = back[64:128].astype(bf16)
             return carry
 
-        lax.fori_loop(0, NC // BLK, cells, 0)
+        for i in range(NC // BLK):
+            cells(i, 0)
 
         def backward_faces(i, carry):
-            at = pl.ds(pl.multiple_of(i * BLK, BLK), BLK)
+            at = pl.ds(pl.multiple_of(i * BLK, BLK), BLK) if not isinstance(i, int) else slice(i * BLK, i * BLK + BLK)
             lo, hi = split_index(rcv[:, at])
             cotangent = ect[:, at].astype(f32)
             upstream = cotangent
@@ -324,7 +328,8 @@
             dedges[:, at] = (cotangent + mm(w1[128:192, :], hidden)).astype(bf16)
             return carry
 
-        lax.fori_loop(0, NF // BLK, backward_faces, 0)
+        for i in range(NF // BLK):
+            backward_faces(i, 0)
 
         edge_part = mm_last(stk[...], ehd[...])
         node_part = mm_last(nin[...], nh2[...])
@@ -359,7 +364,7 @@
         acc[...] = jnp.zeros_like(acc)
 
         def sum_ghosts(i, carry):
-            at = pl.ds(pl.multiple_of(i * BLK, BLK), BLK)
+            at = pl.ds(pl.multiple_of(i * BLK, BLK), BLK) if not isinstance(i, int) else slice(i * BLK, i * BLK + BLK)
             lo, hi = col_s[at, 0:128], col_s[at, 128:256]
             part = ehd[0:64, at]
             for tile in range(6):
@@ -367,7 +372,8 @@
                 acc[:, where] += mm(part, selector_t(lo, hi, 4 + tile, iotas))
             return carry
 
-        lax.fori_loop(0, NF // BLK, sum_ghosts, 0)
+        for i in range(NF // BLK):
+            sum_ghosts(i, 0)
         for pair in range(NB // 2):
             block = mm(
                 w1[0:64, :], acc[:, 256 * pair : 256 * pair + 256].astype(bf16)
@@ -424,7 +430,7 @@
         gt[...] = jnp.zeros_like(gt)
 
         def sum_own(i, carry):
-            at = pl.ds(pl.multiple_of(i * BLK, BLK), BLK)
+            at = pl.ds(pl.multiple_of(i * BLK, BLK), BLK) if not isinstance(i, int) else slice(i * BLK, i * BLK + BLK)
             part = ehd[0:64, at]
             for cols, total in ((col_s, acc), (col_r, gt)):
                 lo, hi = cols[at, 0:128], cols[at, 128:256]
@@ -433,7 +439,8 @@
                     total[:, where] += mm(part, selector_t(lo, hi, tile, iotas))
             return carry
 
-        lax.fori_loop(0, NF // BLK, sum_own, 0)
+        for i in range(NF // BLK):
+            sum_own(i, 0)
         own[...] += mm(w1[0:64, :], acc[:, 0:NC].astype(bf16)) + mm(
             w1[64:128, :], gt[...].astype(bf16)
         )
@@ -609,7 +616,7 @@
         scratch_shapes=scratch,
         compiler_params=pltpu.CompilerParams(**params),
         name="layer",
-    )(*args)
+    )(*[pltpu.with_memory_space_constraint(arg, pltpu.HBM) for arg in args])
     return pl.pallas_call(
         finish,
         out_shape=[jax.ShapeDtypeStruct(shape, kind) for shape, kind in shapes],

time: 55.3 us -> 42.8 us (0.77)
  local copies, waits for them, and re-layouts: 8.77 us -> 0 us
  Pallas kernels: 45.2 us -> 41.9 us
    unnamed x32 -> x0, local copies, waits for them, and re-layouts: 8.77 us -> none
    pallas_call x1, Pallas kernels: 44.2 us -> 40.9 us  [call(): pl.pallas_call(make_kernel(comm), out_shape=[jax.ShapeDtypeStruct(shape,...]
where the time goes in v3:
time: 42.8 us; the launch traced here: 42.7 us
  Pallas kernels  41.9 us (98%)
  between operations  0.82 us (2%)
    pallas_call x1, Pallas kernels, call(): pl.pallas_call(make_kernel(comm), out_shape=[jax.ShapeDtypeStruct(shape,...  40.9 us
    pallas_call x1, Pallas kernels, call(): pl.pallas_call(finish, out_shape=[jax.ShapeDtypeStruct(shape, kind) for s...  0.96 us

profile of v3, /device:TPU:1, one launch (start us, length us, event | category | flops | bytes accessed | tf_op | source)
XLA Modules:
  0.0 42.7 jit_solution(12357806711086381386)
XLA Ops:
  0.7 40.9 %layer.1 = (bf16[64,1024]{1,0:T(8,128)(2,1)S(1)}, bf16[64,3072]{1,0:T(8,128)(2,1)S(1)}, f32[256,128]{1,0:T(8,128)S(1)}) custom-call(bf16[64,1024]{1,0:T(8,128)(2,1)} %refs_0_.1, bf16[64,3072]{1,0:T(8,128)(2,1)} %refs_1_.1, s32[1,3072]{1,0:T(1,128)} %bitcast.20, s32[1,3072]{1,0:T(1,128)} %bitcast.21, s32[1,1536]{1,0:T(1,128)} %bitcast.22, ...), custom_call_target="tpu_custom_call" | custom-call | tf_op jit(solution)/shard_map/layer/pallas_call | solution.py:609
  41.6 1.0 %finish.1 = (bf16[64,1024]{1,0:T(8,128)(2,1)}, bf16[64,3072]{1,0:T(8,128)(2,1)}, f32[64,192]{1,0:T(8,128)}, f32[1,64]{1,0:T(1,128)}, f32[64,64]{1,0:T(8,128)}, /...) custom-call(bf16[64,1024]{1,0:T(8,128)(2,1)S(1)} %get-tuple-element., ...), custom_call_target="tpu_custom_call" | custom-call | tf_op jit(solution)/shard_map/finish/pallas_call | solution.py:620

commit v4 on v2

v4 whole, which is shorter than its diff:
```python
import math

import jax
import jax.numpy as jnp
from jax import lax
from jax.experimental import pallas as pl
from jax.experimental.pallas import tpu as pltpu
from jax.sharding import Mesh
from jax.sharding import PartitionSpec as P

AXES = ("z", "y", "core", "sub")
MESH = pl.DeviceIdType.MESH
EPSILON = 1e-05
D = 64
NF = 3072
NC = 1024
NB = 12
HALO = 128
BLK = 512
bf16 = jnp.bfloat16
f32 = jnp.float32
i16 = jnp.int16
FACTOR = 1.0 / math.sqrt(393216)


def mm(a, b):
    return jnp.dot(a, b, preferred_element_type=f32)


def mm_last(a, b):
    return lax.dot_general(a, b, (((1,), (1,)), ((), ())), preferred_element_type=f32)


def rows_of(index):
    return jnp.broadcast_to(index, (16, index.shape[1])).astype(i16)


def selector(rows, tile):
    width = rows.shape[1]
    iota = lax.broadcasted_iota(jnp.int32, (256, 128), 0).astype(i16)
    iota = jnp.concatenate([iota] * (width // 128), axis=1)
    key = jnp.concatenate([rows - i16(256 * tile)] * 16, axis=0)
    return jnp.where(iota == key, bf16(1), bf16(0))


def columns_of(index):
    width = index.shape[1]
    sub = lax.broadcasted_iota(jnp.int32, (8, width), 0)
    low, high = index & 255, index >> 8
    parts = jnp.where(sub == 0, low, jnp.where(sub == 1, high, 0)).astype(f32)
    sub = lax.broadcasted_iota(jnp.int32, (8, 128), 0)
    scale = jnp.where(sub == 0, 1.0, jnp.where(sub == 1, 256.0, 0.0))
    out = lax.dot_general(parts, scale, (((0,), (0,)), ((), ())), preferred_element_type=f32)
    return out.astype(jnp.int32).astype(i16)


def selector_t(column, tile):
    lane = lax.broadcasted_iota(jnp.int32, (16, 128), 1).astype(i16)
    halves = []
    for half in range(2):
        key = jnp.concatenate([lane + i16(256 * tile + 128 * half)] * (column.shape[0] // 16), axis=0)
        halves.append(jnp.where(column == key, bf16(1), bf16(0)))
    return jnp.concatenate(halves, axis=1)


def staged(stages, count):
    for step in range(count + len(stages) - 1):
        for depth, stage in enumerate(stages):
            if 0 <= step - depth < count:
                stage(step - depth)


def block_at(i):
    return slice(i * BLK, i * BLK + BLK)


def column_of(row):
    sub = lax.broadcasted_iota(jnp.int32, (D, D), 0)
    lane = lax.broadcasted_iota(jnp.int32, (D, D), 1)
    col = jnp.sum(jnp.where(sub == lane, row, 0.0), axis=1, keepdims=True)
    return jnp.broadcast_to(col, (D, 128))


def wide(col, width):
    return jnp.concatenate([col] * (width // 128), axis=1)


def fold_lanes(values):
    total = values[:, 0:128]
    for begin in range(128, values.shape[1], 128):
        total = total + values[:, begin : begin + 128]
    return total


def mean_rows(values):
    return jnp.sum(values, axis=0, keepdims=True) * (1.0 / D)


def logistic(values):
    return 0.5 * jnp.tanh(0.5 * values) + 0.5


def standardize(values):
    centered = values - mean_rows(values)
    spread = lax.rsqrt(mean_rows(centered * centered) + EPSILON)
    return centered * spread, spread


def normalize_back(upstream, scaled, spread, gain):
    weighted = upstream * gain
    return spread * (weighted - mean_rows(weighted) - scaled * mean_rows(weighted * scaled))


def make_kernel(comm):
    def kernel(
        *refs
    ):
        given, refs = refs[:16], refs[16:]
        (dstate, dedges, packed), refs = refs[:3], refs[3:]
        held, refs = refs[:16], refs[16:]
        (
            stk, slope, scl, ups, spr, msg, ehd, col_s, col_r, col_p,
            sendb, ghost, gsend, gback, nin, nh2, nbr, own, acc, gac, gt,
            vec, sums, grads, shared, rs_buf, ex_buf, ag_buf, w1, w2t, nw1, nw2t,
            sem_fs, sem_fr, sem_bs, sem_br, sem_rs, sem_rr, sem_es, sem_er, sem_as, sem_ar,
            sem_in,
        ) = refs
        ns, es, snd, rcv, six, nct, ect, w1t, b1, w2, eg, esh, nw1t, nb1, nw2, ng = held
        loads = [
            pltpu.make_async_copy(given[k], held[k], sem_in.at[k]) for k in range(16)
        ]
        for k in (4, 0, 2, 3, 1, 7, 8, 9, 10, 11, 12, 13, 14, 15, 5, 6):
            loads[k].start()
        if comm:
            z = lax.axis_index("z")
            y = lax.axis_index("y")
            core = lax.axis_index("core")
            s = lax.axis_index("sub")
            d = z * 8 + y * 2 + core
            a = z * 2 + core
            b = y * 4 + s

            def row_peer(step, t):
                dd = lax.rem(d + (step + 32), 32)
                return lax.div(dd, 8), lax.rem(lax.div(dd, 2), 4), lax.rem(dd, 2), t

            def a_peer(j):
                other = lax.rem(a + j, 8)
                return other, (lax.div(other, 2), y, lax.rem(other, 2), s)

            def b_peer(j):
                other = lax.rem(b + j, 16)
                return other, (z, lax.div(other, 4), core, lax.rem(other, 4))

            halo_pairs = [(o, r) for o in range(3) for r in range(4) if not (o == 1 and r == 0)]
            barrier = pltpu.get_barrier_semaphore()
            peers = [row_peer(o - 1, lax.rem(s + r, 4)) for o, r in halo_pairs]
            peers += [a_peer(j)[1] for j in range(1, 8)] + [b_peer(j)[1] for j in range(1, 16)]
            for peer in peers:
                pl.semaphore_signal(barrier, inc=1, device_id=peer, device_id_type=MESH)
        else:
            s = 0

        def waits(copies):
            for condition, copy in copies:
                if condition is None:
                    copy.wait_send()
                else:
                    pl.when(condition)(copy.wait_send)

        def send_block(k, source, target, sems, turn):
            o, t = k // 4, k % 4
            copy = pltpu.make_async_remote_copy(
                src_ref=source.at[k],
                dst_ref=target.at[o * 4 + s],
                send_sem=sems[0].at[k],
                recv_sem=sems[1].at[o * 4 + s],
                device_id=row_peer(turn * (o - 1), t),
                device_id_type=MESH,
            )
            condition = s != t if o == 1 else None
            if condition is None:
                copy.start()
            else:
                pl.when(condition)(copy.start)
            return condition, copy

        def receive_blocks(source, target, sems):
            for o, r in halo_pairs:
                slot = o * 4 + lax.rem(s + r, 4)
                pltpu.make_async_remote_copy(
                    src_ref=source.at[slot],
                    dst_ref=target.at[slot],
                    send_sem=sems[0].at[0],
                    recv_sem=sems[1].at[slot],
                    device_id=row_peer(o - 1, lax.rem(s + r, 4)),
                    device_id_type=MESH,
                ).wait_recv()

        loads[4].wait()
        loads[0].wait()
        forward = []
        for place, pair in enumerate((0, 1, 4, 5, 2, 3)):
            rows = rows_of(six[:, 256 * pair : 256 * pair + 256])
            picked = jnp.zeros((D, 256), f32)
            for tile in range(4):
                picked = picked + mm(ns[:, 256 * tile : 256 * tile + 256], selector(rows, tile))
            picked = picked.astype(bf16)
            sendb[2 * pair] = picked[:, :HALO]
            sendb[2 * pair + 1] = picked[:, HALO:]
            if comm:
                if place == 0:
                    pl.semaphore_wait(barrier, len(peers))
                for k in (2 * pair, 2 * pair + 1):
                    forward.append(send_block(k, sendb, ghost, (sem_fs, sem_fr), 1))

        ghost[4 + s] = jnp.zeros((D, HALO), bf16)
        gback[4 + s] = jnp.zeros((D, HALO), bf16)
        for k in (2, 3, 1, 7, 8, 9, 10, 11, 12, 13, 14, 15):
            loads[k].wait()
        vec[0] = column_of(b1[...])
        vec[1] = column_of(eg[...])
        vec[2] = column_of(esh[...])
        vec[3] = column_of(nb1[...])
        vec[4] = column_of(ng[...])
        w1[...] = w1t[...].astype(f32).T.astype(bf16)
        w2t[...] = w2[...].astype(f32).T.astype(bf16)
        nw1[...] = nw1t[...].astype(f32).T.astype(bf16)
        nw2t[...] = nw2[...].astype(f32).T.astype(bf16)
        sums[...] = jnp.zeros_like(sums)
        stk[128:192, :] = es[...]
        nin[0:64, :] = ns[...]

        def gather_own(i):
            at = block_at(i)
            for index, begin in ((snd, 0), (rcv, 64)):
                rows = rows_of(index[:, at])
                total = jnp.zeros((D, BLK), f32)
                for tile in range(4):
                    total = total + mm(ns[:, 256 * tile : 256 * tile + 256], selector(rows, tile))
                stk[begin : begin + 64, at] = total.astype(bf16)
            col_s[at, :] = columns_of(snd[:, at])
            col_r[at, :] = columns_of(rcv[:, at])

        staged([gather_own], NF // BLK)
        for pair in range(NB // 2):
            at = slice(256 * pair, 256 * pair + 256)
            col_p[at, :] = columns_of(six[:, at])

        if comm:
            receive_blocks(sendb, ghost, (sem_fs, sem_fr))

        def gather_ghosts(i):
            at = block_at(i)
            rows = rows_of(snd[:, at])
            total = stk[0:64, at].astype(f32)
            for pair in range(NB // 2):
                table = jnp.concatenate([ghost[2 * pair], ghost[2 * pair + 1]], axis=1)
                total = total + mm(table, selector(rows, 4 + pair))
            stk[0:64, at] = total.astype(bf16)

        def forward_faces(i):
            at = block_at(i)
            linear = mm(w1t[...], stk[0:192, at]) + wide(vec[0], BLK)
            gate = logistic(linear)
            activated = linear * gate
            active = activated.astype(bf16)
            stk[192:256, at] = active
            slope[:, at] = gate + activated * (1.0 - gate)
            scaled, spread = standardize(mm(w2t[...], active))
            scl[:, at] = scaled
            spr[:, at] = spread
            msg[:, at] = (scaled * wide(vec[1], BLK) + wide(vec[2], BLK)).astype(bf16)

        def scatter(i, part, column, total, tiles, first):
            for tile in tiles:
                where = slice(256 * (tile - tiles[0]), 256 * (tile - tiles[0]) + 256)
                added = mm(part, selector_t(column, tile))
                total[:, where] = added if first else total[:, where] + added

        def sum_messages(i):
            at = block_at(i)
            scatter(i, msg[:, at], col_r[at, :], acc, range(4), i == 0)

        staged([gather_ghosts, forward_faces, sum_messages], NF // BLK)

        loads[5].wait()
        loads[6].wait()
        def cells(i):
            at = block_at(i)
            nin[64:128, at] = acc[:, at].astype(bf16)
            linear = mm(nw1t[...], nin[0:128, at]) + wide(vec[3], BLK)
            gate = logistic(linear)
            activated = linear * gate
            active = activated.astype(bf16)
            nin[128:192, at] = active
            scaled, spread = standardize(mm(nw2t[...], active))
            upstream = nct[:, at].astype(f32)
            sums[4] += fold_lanes(upstream * scaled)
            sums[5] += fold_lanes(upstream)
            delta = normalize_back(upstream, scaled, spread, wide(vec[4], BLK)).astype(bf16)
            nh2[0:64, at] = delta
            hidden = mm(nw2[...], delta) * (gate + activated * (1.0 - gate))
            sums[3] += fold_lanes(hidden)
            hidden = hidden.astype(bf16)
            nh2[64:128, at] = hidden
            back = mm(nw1[...], hidden)
            own[:, at] = back[0:64] + upstream
            nbr[:, at] = back[64:128].astype(bf16)

        staged([cells], NC // BLK)

        def gather_back(i):
            at = block_at(i)
            rows = rows_of(rcv[:, at])
            upstream = ect[:, at].astype(f32)
            for tile in range(4):
                upstream = upstream + mm(
                    nbr[:, 256 * tile : 256 * tile + 256], selector(rows, tile)
                )
            ups[:, at] = upstream

        def backward_faces(i):
            at = block_at(i)
            upstream = ups[:, at]
            scaled = scl[:, at]
            sums[1] += fold_lanes(upstream * scaled)
            sums[2] += fold_lanes(upstream)
            delta = normalize_back(upstream, scaled, spr[:, at], wide(vec[1], BLK)).astype(bf16)
            ehd[64:128, at] = delta
            hidden = mm(w2[...], delta) * slope[:, at]
            sums[0] += fold_lanes(hidden)
            ehd[0:64, at] = hidden.astype(bf16)

        def sum_ghosts(i):
            at = block_at(i)
            scatter(i, ehd[0:64, at], col_s[at, :], gac, range(4, 10), i == 0)

        staged([gather_back, backward_faces, sum_ghosts], NF // BLK)

        edge_part = mm_last(stk[...], ehd[...])
        node_part = mm_last(nin[...], nh2[...])
        lane64 = lax.broadcasted_iota(jnp.int32, (64, 128), 1)
        vectors = jnp.zeros((64, 128), f32)
        for number in range(6):
            vectors = jnp.where(
                lane64 == 64 + number, jnp.sum(sums[number], axis=1, keepdims=True), vectors
            )
        high = vectors.astype(bf16).astype(f32)
        vectors = high + pltpu.roll(vectors - high, 6, 1)
        grads[0:64] = jnp.where(lane64 < 64, edge_part[0:64], node_part[0:64])
        grads[64:128] = jnp.where(lane64 < 64, edge_part[64:128], node_part[64:128])
        grads[128:192] = jnp.where(lane64 < 64, edge_part[128:192], vectors)
        grads[192:256] = jnp.where(lane64 < 64, node_part[128:192], edge_part[192:256])

        first = []
        if comm:
            shared[...] = grads[...].astype(bf16)
            for j in range(1, 8):
                other, peer = a_peer(j)
                first.append(
                    pltpu.make_async_remote_copy(
                        src_ref=shared.at[pl.ds(pl.multiple_of(other * 32, 32), 32), :],
                        dst_ref=rs_buf.at[a],
                        send_sem=sem_rs.at[j],
                        recv_sem=sem_rr.at[a],
                        device_id=peer,
                        device_id_type=MESH,
                    )
                )
            for copy in first:
                copy.start()

        backward = []
        for pair in (0, 1, 4, 5, 2, 3):
            block = mm(w1[0:64, :], gac[:, 256 * pair : 256 * pair + 256].astype(bf16)).astype(bf16)
            gsend[2 * pair] = block[:, :HALO]
            gsend[2 * pair + 1] = block[:, HALO:]
            if comm:
                for k in (2 * pair, 2 * pair + 1):
                    backward.append(send_block(k, gsend, gback, (sem_bs, sem_br), -1))

        for i in range(NF // BLK):
            at = block_at(i)
            dedges[:, at] = (ect[:, at].astype(f32) + mm(w1[128:192, :], ehd[0:64, at])).astype(bf16)

        def split_vectors(total):
            lane = lax.broadcasted_iota(jnp.int32, (32, 128), 1)
            whole = total + pltpu.roll(total, 122, 1)
            high = whole.astype(bf16).astype(f32)
            parts = jnp.where(lane < 70, high, pltpu.roll(whole - high, 6, 1))
            return jnp.where(((a == 4) | (a == 5)) & (lane >= 64) & (lane < 76), parts, total)

        second = []
        if comm:
            total = grads[pl.ds(pl.multiple_of(a * 32, 32), 32), :]
            for j in range(1, 8):
                other, peer = a_peer(j)
                pltpu.make_async_remote_copy(
                    src_ref=rs_buf.at[other],
                    dst_ref=rs_buf.at[other],
                    send_sem=sem_rs.at[j],
                    recv_sem=sem_rr.at[other],
                    device_id=peer,
                    device_id_type=MESH,
                ).wait_recv()
                total = total + rs_buf[other].astype(f32)
            ex_buf[b] = split_vectors(total).astype(bf16)
            for j in range(1, 16):
                other, peer = b_peer(j)
                second.append(
                    pltpu.make_async_remote_copy(
                        src_ref=ex_buf.at[b],
                        dst_ref=ex_buf.at[b],
                        send_sem=sem_es.at[j],
                        recv_sem=sem_er.at[b],
                        device_id=peer,
                        device_id_type=MESH,
                    )
                )
            for copy in second:
                copy.start()

        def sum_own(i):
            at = block_at(i)
            scatter(i, ehd[0:64, at], col_s[at, :], acc, range(4), i == 0)
            scatter(i, ehd[0:64, at], col_r[at, :], gt, range(4), i == 0)

        staged([sum_own], NF // BLK)
        own[...] += mm(w1[0:64, :], acc[...].astype(bf16)) + mm(w1[64:128, :], gt[...].astype(bf16))

        third = []
        if comm:
            for j in range(1, 16):
                other, peer = b_peer(j)
                pltpu.make_async_remote_copy(
                    src_ref=ex_buf.at[other],
                    dst_ref=ex_buf.at[other],
                    send_sem=sem_es.at[j],
                    recv_sem=sem_er.at[other],
                    device_id=peer,
                    device_id_type=MESH,
                ).wait_recv()
            total = ex_buf[0].astype(f32)
            for j in range(1, 16):
                total = total + ex_buf[j].astype(f32)
            ag_buf[a] = split_vectors(total).astype(bf16)
            for j in range(1, 8):
                other, peer = a_peer(j)
                third.append(
                    pltpu.make_async_remote_copy(
                        src_ref=ag_buf.at[a],
                        dst_ref=ag_buf.at[a],
                        send_sem=sem_as.at[j],
                        recv_sem=sem_ar.at[a],
                        device_id=peer,
                        device_id_type=MESH,
                    )
                )
            for copy in third:
                copy.start()

            receive_blocks(gsend, gback, (sem_bs, sem_br))

        returned = jnp.concatenate([gback[k] for k in range(NB)], axis=1)
        for tile in range(4):
            where = slice(256 * tile, 256 * tile + 256)
            total = own[:, where]
            for pair in range(NB // 2):
                at = slice(256 * pair, 256 * pair + 256)
                total = total + mm(returned[:, at], selector_t(col_p[at, :], tile))
            dstate[:, where] = total.astype(bf16)

        if comm:
            for j in range(1, 8):
                other, peer = a_peer(j)
                pltpu.make_async_remote_copy(
                    src_ref=ag_buf.at[other],
                    dst_ref=ag_buf.at[other],
                    send_sem=sem_as.at[j],
                    recv_sem=sem_ar.at[other],
                    device_id=peer,
                    device_id_type=MESH,
                ).wait_recv()
            for j in range(8):
                packed[32 * j : 32 * j + 32] = ag_buf[j].astype(f32)
        else:
            packed[...] = grads[...]
        waits(forward + backward)
        for copy in first + second + third:
            copy.wait_send()

    return kernel


def finish(
    dstate, dedges, packed, out_state, out_edges, *refs
):
    results, refs = refs[:10], refs[10:]
    staged, sems = refs[:10], refs[10]
    o_w1, o_b1, o_w2, o_eg, o_es, o_nw1, o_nb1, o_nw2, o_ng, o_ns = staged
    stores = [
        pltpu.make_async_copy(dedges, out_edges, sems.at[10]),
        pltpu.make_async_copy(dstate, out_state, sems.at[11]),
    ]
    for copy in stores:
        copy.start()
    whole = packed[...] * FACTOR
    turned = jnp.concatenate([whole[0:128].T, whole[128:256].T], axis=1)
    o_w1[...] = turned[0:64, 0:192]
    o_nw1[...] = turned[64:128, 0:128]
    o_nw2[...] = whole[192:256, 0:64]
    o_w2[...] = pltpu.roll(whole[192:256], 64, 1)[:, 0:64]
    rows = turned[64:128, 128:192]
    for k, ref in enumerate((o_b1, o_eg, o_es, o_nb1, o_ng, o_ns)):
        ref[...] = rows[k : k + 1, :] + rows[k + 6 : k + 7, :]
    for k in range(10):
        copy = pltpu.make_async_copy(staged[k], results[k], sems.at[k])
        copy.start()
        stores.append(copy)
    for copy in stores:
        copy.wait()


def call(comm, *args):
    shapes = [
        ((D, NC), bf16),
        ((D, NF), bf16),
        ((64, 192), f32),
        ((1, 64), f32),
        ((64, 64), f32),
        ((1, 64), f32),
        ((1, 64), f32),
        ((64, 128), f32),
        ((1, 64), f32),
        ((64, 64), f32),
        ((1, 64), f32),
        ((1, 64), f32),
    ]
    dma = pltpu.SemaphoreType.DMA
    scratch = [pltpu.VMEM(arg.shape, arg.dtype) for arg in args]
    scratch += [
        pltpu.VMEM((256, NF), bf16),
        pltpu.VMEM((D, NF), f32),
        pltpu.VMEM((D, NF), f32),
        pltpu.VMEM((D, NF), f32),
        pltpu.VMEM((1, NF), f32),
        pltpu.VMEM((D, NF), bf16),
        pltpu.VMEM((128, NF), bf16),
        pltpu.VMEM((NF, 128), i16),
        pltpu.VMEM((NF, 128), i16),
        pltpu.VMEM((NB * HALO, 128), i16),
        pltpu.VMEM((NB, D, HALO), bf16),
        pltpu.VMEM((NB, D, HALO), bf16),
        pltpu.VMEM((NB, D, HALO), bf16),
        pltpu.VMEM((NB, D, HALO), bf16),
        pltpu.VMEM((192, NC), bf16),
        pltpu.VMEM((128, NC), bf16),
        pltpu.VMEM((D, NC), bf16),
        pltpu.VMEM((D, NC), f32),
        pltpu.VMEM((D, NC), f32),
        pltpu.VMEM((D, NB * HALO), f32),
        pltpu.VMEM((D, NC), f32),
        pltpu.VMEM((5, D, 128), f32),
        pltpu.VMEM((6, D, 128), f32),
        pltpu.VMEM((256, 128), f32),
        pltpu.VMEM((256, 128), bf16),
        pltpu.VMEM((8, 32, 128), bf16),
        pltpu.VMEM((16, 32, 128), bf16),
        pltpu.VMEM((8, 32, 128), bf16),
        pltpu.VMEM((192, 64), bf16),
        pltpu.VMEM((64, 64), bf16),
        pltpu.VMEM((128, 64), bf16),
        pltpu.VMEM((64, 64), bf16),
        dma((12,)), dma((12,)), dma((12,)), dma((12,)),
        dma((8,)), dma((8,)), dma((16,)), dma((16,)), dma((8,)), dma((8,)),
        dma((16,)),
    ]
    anywhere = pl.BlockSpec(memory_space=pltpu.HBM)
    params = dict(vmem_limit_bytes=36 * 1024 * 1024)
    if comm:
        params.update(collective_id=0, has_side_effects=True)
    vmem = pl.BlockSpec(memory_space=pltpu.VMEM)
    middle = pl.pallas_call(
        make_kernel(comm),
        out_shape=[
            jax.ShapeDtypeStruct(shape, kind) for shape, kind in shapes[:2] + [((256, 128), f32)]
        ],
        in_specs=[anywhere] * 16,
        out_specs=[vmem] * 3,
        scratch_shapes=scratch,
        compiler_params=pltpu.CompilerParams(**params),
        name="layer",
    )(*[pltpu.with_memory_space_constraint(arg, pltpu.HBM) for arg in args])
    return pl.pallas_call(
        finish,
        out_shape=[jax.ShapeDtypeStruct(shape, kind) for shape, kind in shapes],
        in_specs=[vmem] * 3,
        out_specs=[anywhere] * 12,
        scratch_shapes=[pltpu.VMEM(shape, kind) for shape, kind in shapes[2:]] + [dma((12,))],
        compiler_params=pltpu.CompilerParams(vmem_limit_bytes=8 * 1024 * 1024),
        name="finish",
    )(*middle)


def on_device(comm, node_state, edge_state, senders, receivers, send_index, node_cotangent, edge_cotangent,
              edge_first, edge_bias, edge_second, edge_gain, edge_shift, node_first, node_bias, node_second, node_gain):
    line = lambda v: v.reshape(1, -1)
    outs = call(
        comm, node_state, edge_state, line(senders), line(receivers), line(send_index),
        node_cotangent, edge_cotangent, edge_first.T, line(edge_bias), edge_second, line(edge_gain),
        line(edge_shift), node_first.T, line(node_bias), node_second, line(node_gain),
    )
    outs = [v.reshape(-1) if v.shape[0] == 1 else v for v in outs]
    outs[2] = outs[2].T
    outs[7] = outs[7].T
    return tuple(outs)


def solution(mesh):
    split = Mesh(mesh.devices.reshape(4, 4, 2, 4), AXES)
    every = P(None, AXES)
    in_specs = (every, every, P(AXES), P(AXES), P(AXES, None, None), every, every) + (P(),) * 9
    out_specs = (every, every) + (P(),) * 10
    return jax.shard_map(
        lambda *args: on_device(True, *args), mesh=split, in_specs=in_specs, out_specs=out_specs,
        check_vma=False,
    )
```

time: 55.3 us -> 39.7 us (0.72)
  local copies, waits for them, and re-layouts: 8.77 us -> 0 us
  Pallas kernels: 45.2 us -> 38.8 us
    unnamed x32 -> x0, local copies, waits for them, and re-layouts: 8.77 us -> none
    pallas_call x1, Pallas kernels: 44.2 us -> 37.8 us  [call(): pl.pallas_call(make_kernel(comm), out_shape=[jax.ShapeDtypeStruct(shape,...]
where the time goes in v4:
time: 39.7 us; the launch traced here: 39.6 us
  Pallas kernels  38.8 us (98%)
  between operations  0.82 us (2%)
    pallas_call x1, Pallas kernels, call(): pl.pallas_call(make_kernel(comm), out_shape=[jax.ShapeDtypeStruct(shape,...  37.8 us
    pallas_call x1, Pallas kernels, call(): pl.pallas_call(finish, out_shape=[jax.ShapeDtypeStruct(shape, kind) for s...  0.96 us

profile of v4, /device:TPU:1, one launch (start us, length us, event | category | flops | bytes accessed | tf_op | source)
XLA Modules:
  0.0 39.6 jit_solution(13767194009028948354)
XLA Ops:
  0.7 37.8 %layer.1 = (bf16[64,1024]{1,0:T(8,128)(2,1)S(1)}, bf16[64,3072]{1,0:T(8,128)(2,1)S(1)}, f32[256,128]{1,0:T(8,128)S(1)}) custom-call(bf16[64,1024]{1,0:T(8,128)(2,1)} %refs_0_.1, bf16[64,3072]{1,0:T(8,128)(2,1)} %refs_1_.1, s32[1,3072]{1,0:T(1,128)} %bitcast.20, s32[1,3072]{1,0:T(1,128)} %bitcast.21, s32[1,1536]{1,0:T(1,128)} %bitcast.22, ...), custom_call_target="tpu_custom_call" | custom-call | tf_op jit(solution)/shard_map/layer/pallas_call | solution.py:584
  38.5 1.0 %finish.1 = (bf16[64,1024]{1,0:T(8,128)(2,1)}, bf16[64,3072]{1,0:T(8,128)(2,1)}, f32[64,192]{1,0:T(8,128)}, f32[1,64]{1,0:T(1,128)}, f32[64,64]{1,0:T(8,128)}, /...) custom-call(bf16[64,1024]{1,0:T(8,128)(2,1)S(1)} %get-tuple-element., ...), custom_call_target="tpu_custom_call" | custom-call | tf_op jit(solution)/shard_map/finish/pallas_call | solution.py:595

commit v5 on v4

--- a/solution.py
+++ b/solution.py
@@ -239,13 +239,9 @@
                 for tile in range(4):
                     total = total + mm(ns[:, 256 * tile : 256 * tile + 256], selector(rows, tile))
                 stk[begin : begin + 64, at] = total.astype(bf16)
-            col_s[at, :] = columns_of(snd[:, at])
             col_r[at, :] = columns_of(rcv[:, at])
 
         staged([gather_own], NF // BLK)
-        for pair in range(NB // 2):
-            at = slice(256 * pair, 256 * pair + 256)
-            col_p[at, :] = columns_of(six[:, at])
 
         if comm:
             receive_blocks(sendb, ghost, (sem_fs, sem_fr))
@@ -332,11 +328,7 @@
             sums[0] += fold_lanes(hidden)
             ehd[0:64, at] = hidden.astype(bf16)
 
-        def sum_ghosts(i):
-            at = block_at(i)
-            scatter(i, ehd[0:64, at], col_s[at, :], gac, range(4, 10), i == 0)
-
-        staged([gather_back, backward_faces, sum_ghosts], NF // BLK)
+        staged([gather_back, backward_faces], NF // BLK)
 
         edge_part = mm_last(stk[...], ehd[...])
         node_part = mm_last(nin[...], nh2[...])
@@ -371,18 +363,17 @@
             for copy in first:
                 copy.start()
 
-        backward = []
-        for pair in (0, 1, 4, 5, 2, 3):
-            block = mm(w1[0:64, :], gac[:, 256 * pair : 256 * pair + 256].astype(bf16)).astype(bf16)
-            gsend[2 * pair] = block[:, :HALO]
-            gsend[2 * pair + 1] = block[:, HALO:]
-            if comm:
-                for k in (2 * pair, 2 * pair + 1):
-                    backward.append(send_block(k, gsend, gback, (sem_bs, sem_br), -1))
-
-        for i in range(NF // BLK):
-            at = block_at(i)
-            dedges[:, at] = (ect[:, at].astype(f32) + mm(w1[128:192, :], ehd[0:64, at])).astype(bf16)
+        def sum_ghosts(i):
+            at = block_at(i)
+            col_s[at, :] = columns_of(snd[:, at])
+            scatter(i, ehd[0:64, at], col_s[at, :], gac, range(4, 10), i == 0)
+
+        staged([sum_ghosts], NF // BLK)
+        def sum_senders(i):
+            at = block_at(i)
+            scatter(i, ehd[0:64, at], col_s[at, :], acc, range(4), i == 0)
+
+        staged([sum_senders], NF // BLK)
 
         def split_vectors(total):
             lane = lax.broadcasted_iota(jnp.int32, (32, 128), 1)
@@ -421,13 +412,28 @@
             for copy in second:
                 copy.start()
 
-        def sum_own(i):
-            at = block_at(i)
-            scatter(i, ehd[0:64, at], col_s[at, :], acc, range(4), i == 0)
+        backward = []
+        for pair in (0, 1, 4, 5, 2, 3):
+            block = mm(w1[0:64, :], gac[:, 256 * pair : 256 * pair + 256].astype(bf16)).astype(bf16)
+            gsend[2 * pair] = block[:, :HALO]
+            gsend[2 * pair + 1] = block[:, HALO:]
+            if comm:
+                for k in (2 * pair, 2 * pair + 1):
+                    backward.append(send_block(k, gsend, gback, (sem_bs, sem_br), -1))
+
+        def sum_receivers(i):
+            at = block_at(i)
             scatter(i, ehd[0:64, at], col_r[at, :], gt, range(4), i == 0)
 
-        staged([sum_own], NF // BLK)
+        staged([sum_receivers], NF // BLK)
         own[...] += mm(w1[0:64, :], acc[...].astype(bf16)) + mm(w1[64:128, :], gt[...].astype(bf16))
+        for pair in range(NB // 2):
+            at = slice(256 * pair, 256 * pair + 256)
+            col_p[at, :] = columns_of(six[:, at])
+
+        for i in range(NF // BLK):
+            at = block_at(i)
+            dedges[:, at] = (ect[:, at].astype(f32) + mm(w1[128:192, :], ehd[0:64, at])).astype(bf16)
 
         third = []
         if comm:
@@ -460,6 +466,7 @@
             for copy in third:
                 copy.start()
 
+        if comm:
             receive_blocks(gsend, gback, (sem_bs, sem_br))
 
         returned = jnp.concatenate([gback[k] for k in range(NB)], axis=1)

time: 39.7 us -> 38.1 us (0.960)
  Pallas kernels: 38.8 us -> 37.2 us
    pallas_call x1, Pallas kernels: 37.8 us -> 36.2 us  [call(): pl.pallas_call(make_kernel(comm), out_shape=[jax.ShapeDtypeStruct(shape,...]
where the time goes in v5:
time: 38.1 us; the launch traced here: 38 us
  Pallas kernels  37.2 us (98%)
  between operations  0.82 us (2%)
    pallas_call x1, Pallas kernels, call(): pl.pallas_call(make_kernel(comm), out_shape=[jax.ShapeDtypeStruct(shape,...  36.2 us
    pallas_call x1, Pallas kernels, call(): pl.pallas_call(finish, out_shape=[jax.ShapeDtypeStruct(shape, kind) for s...  0.96 us

profile of v5, /device:TPU:1, one launch (start us, length us, event | category | flops | bytes accessed | tf_op | source)
XLA Modules:
  0.0 38.0 jit_solution(9690635233373556829)
XLA Ops:
  0.7 36.2 %layer.1 = (bf16[64,1024]{1,0:T(8,128)(2,1)S(1)}, bf16[64,3072]{1,0:T(8,128)(2,1)S(1)}, f32[256,128]{1,0:T(8,128)S(1)}) custom-call(bf16[64,1024]{1,0:T(8,128)(2,1)} %refs_0_.1, bf16[64,3072]{1,0:T(8,128)(2,1)} %refs_1_.1, s32[1,3072]{1,0:T(1,128)} %bitcast.20, s32[1,3072]{1,0:T(1,128)} %bitcast.21, s32[1,1536]{1,0:T(1,128)} %bitcast.22, ...), custom_call_target="tpu_custom_call" | custom-call | tf_op jit(solution)/shard_map/layer/pallas_call | solution.py:591
  36.9 1.0 %finish.1 = (bf16[64,1024]{1,0:T(8,128)(2,1)}, bf16[64,3072]{1,0:T(8,128)(2,1)}, f32[64,192]{1,0:T(8,128)}, f32[1,64]{1,0:T(1,128)}, f32[64,64]{1,0:T(8,128)}, /...) custom-call(bf16[64,1024]{1,0:T(8,128)(2,1)S(1)} %get-tuple-element., ...), custom_call_target="tpu_custom_call" | custom-call | tf_op jit(solution)/shard_map/finish/pallas_call | solution.py:602

commit v6 on v5

--- a/solution.py
+++ b/solution.py
@@ -120,8 +120,8 @@
         held, refs = refs[:16], refs[16:]
         (
             stk, slope, scl, ups, spr, msg, ehd, col_s, col_r, col_p,
-            sendb, ghost, gsend, gback, nin, nh2, nbr, own, acc, gac, gt,
-            vec, sums, grads, shared, rs_buf, ex_buf, ag_buf, w1, w2t, nw1, nw2t,
+            sendb, ghost, gsend, gback, nin, nh2, nbr, own, nslope, acc, gac, gt,
+            vec, sums, grads, eacc, shared, rs_buf, ex_buf, ag_buf, w1, w2t, nw1, nw2t,
             sem_fs, sem_fr, sem_bs, sem_br, sem_rs, sem_rr, sem_es, sem_er, sem_as, sem_ar,
             sem_in,
         ) = refs
@@ -240,8 +240,12 @@
                     total = total + mm(ns[:, 256 * tile : 256 * tile + 256], selector(rows, tile))
                 stk[begin : begin + 64, at] = total.astype(bf16)
             col_r[at, :] = columns_of(rcv[:, at])
+            col_s[at, :] = columns_of(snd[:, at])
 
         staged([gather_own], NF // BLK)
+        for pair in range(NB // 2):
+            at = slice(256 * pair, 256 * pair + 256)
+            col_p[at, :] = columns_of(six[:, at])
 
         if comm:
             receive_blocks(sendb, ghost, (sem_fs, sem_fr))
@@ -263,7 +267,10 @@
             active = activated.astype(bf16)
             stk[192:256, at] = active
             slope[:, at] = gate + activated * (1.0 - gate)
-            scaled, spread = standardize(mm(w2t[...], active))
+
+        def forward_norms(i):
+            at = block_at(i)
+            scaled, spread = standardize(mm(w2t[...], stk[192:256, at]))
             scl[:, at] = scaled
             spr[:, at] = spread
             msg[:, at] = (scaled * wide(vec[1], BLK) + wide(vec[2], BLK)).astype(bf16)
@@ -278,7 +285,7 @@
             at = block_at(i)
             scatter(i, msg[:, at], col_r[at, :], acc, range(4), i == 0)
 
-        staged([gather_ghosts, forward_faces, sum_messages], NF // BLK)
+        staged([gather_ghosts, forward_faces, forward_norms, sum_messages], NF // BLK)
 
         loads[5].wait()
         loads[6].wait()
@@ -290,13 +297,21 @@
             activated = linear * gate
             active = activated.astype(bf16)
             nin[128:192, at] = active
-            scaled, spread = standardize(mm(nw2t[...], active))
+            nslope[:, at] = gate + activated * (1.0 - gate)
+
+        def cell_norms(i):
+            at = block_at(i)
+            scaled, spread = standardize(mm(nw2t[...], nin[128:192, at]))
             upstream = nct[:, at].astype(f32)
             sums[4] += fold_lanes(upstream * scaled)
             sums[5] += fold_lanes(upstream)
             delta = normalize_back(upstream, scaled, spread, wide(vec[4], BLK)).astype(bf16)
             nh2[0:64, at] = delta
-            hidden = mm(nw2[...], delta) * (gate + activated * (1.0 - gate))
+
+        def cell_hidden(i):
+            at = block_at(i)
+            upstream = nct[:, at].astype(f32)
+            hidden = mm(nw2[...], nh2[0:64, at]) * nslope[:, at]
             sums[3] += fold_lanes(hidden)
             hidden = hidden.astype(bf16)
             nh2[64:128, at] = hidden
@@ -304,7 +319,7 @@
             own[:, at] = back[0:64] + upstream
             nbr[:, at] = back[64:128].astype(bf16)
 
-        staged([cells], NC // BLK)
+        staged([cells, cell_norms, cell_hidden], NC // BLK)
 
         def gather_back(i):
             at = block_at(i)
@@ -324,13 +339,21 @@
             sums[2] += fold_lanes(upstream)
             delta = normalize_back(upstream, scaled, spr[:, at], wide(vec[1], BLK)).astype(bf16)
             ehd[64:128, at] = delta
-            hidden = mm(w2[...], delta) * slope[:, at]
+
+        def backward_hidden(i):
+            at = block_at(i)
+            hidden = mm(w2[...], ehd[64:128, at]) * slope[:, at]
             sums[0] += fold_lanes(hidden)
             ehd[0:64, at] = hidden.astype(bf16)
 
-        staged([gather_back, backward_faces], NF // BLK)
-
-        edge_part = mm_last(stk[...], ehd[...])
+        def weigh_faces(i):
+            at = block_at(i)
+            part = mm_last(stk[:, at], ehd[:, at])
+            eacc[...] = part if i == 0 else eacc[...] + part
+
+        staged([gather_back, backward_faces, backward_hidden, weigh_faces], NF // BLK)
+
+        edge_part = eacc[...]
         node_part = mm_last(nin[...], nh2[...])
         lane64 = lax.broadcasted_iota(jnp.int32, (64, 128), 1)
         vectors = jnp.zeros((64, 128), f32)
@@ -365,7 +388,6 @@
 
         def sum_ghosts(i):
             at = block_at(i)
-            col_s[at, :] = columns_of(snd[:, at])
             scatter(i, ehd[0:64, at], col_s[at, :], gac, range(4, 10), i == 0)
 
         staged([sum_ghosts], NF // BLK)
@@ -427,9 +449,6 @@
 
         staged([sum_receivers], NF // BLK)
         own[...] += mm(w1[0:64, :], acc[...].astype(bf16)) + mm(w1[64:128, :], gt[...].astype(bf16))
-        for pair in range(NB // 2):
-            at = slice(256 * pair, 256 * pair + 256)
-            col_p[at, :] = columns_of(six[:, at])
 
         for i in range(NF // BLK):
             at = block_at(i)
@@ -566,10 +585,12 @@
         pltpu.VMEM((D, NC), bf16),
         pltpu.VMEM((D, NC), f32),
         pltpu.VMEM((D, NC), f32),
+        pltpu.VMEM((D, NC), f32),
         pltpu.VMEM((D, NB * HALO), f32),
         pltpu.VMEM((D, NC), f32),
         pltpu.VMEM((5, D, 128), f32),
         pltpu.VMEM((6, D, 128), f32),
+        pltpu.VMEM((256, 128), f32),
         pltpu.VMEM((256, 128), f32),
         pltpu.VMEM((256, 128), bf16),
         pltpu.VMEM((8, 32, 128), bf16),

time: 38.1 us -> 36.6 us (0.961)
  Pallas kernels: 37.2 us -> 35.6 us
    pallas_call x1, Pallas kernels: 36.2 us -> 34.7 us  [call(): pl.pallas_call(make_kernel(comm), out_shape=[jax.ShapeDtypeStruct(shape,...]
where the time goes in v6:
time: 36.6 us; the launch traced here: 36.4 us
  Pallas kernels  35.6 us (97%)
  between operations  0.82 us (2%)
    pallas_call x1, Pallas kernels, call(): pl.pallas_call(make_kernel(comm), out_shape=[jax.ShapeDtypeStruct(shape,...  34.7 us
    pallas_call x1, Pallas kernels, call(): pl.pallas_call(finish, out_shape=[jax.ShapeDtypeStruct(shape, kind) for s...  0.96 us

profile of v6, /device:TPU:1, one launch (start us, length us, event | category | flops | bytes accessed | tf_op | source)
XLA Modules:
  0.0 36.4 jit_solution(4549524450289867725)
XLA Ops:
  0.7 34.7 %layer.1 = (bf16[64,1024]{1,0:T(8,128)(2,1)S(1)}, bf16[64,3072]{1,0:T(8,128)(2,1)S(1)}, f32[256,128]{1,0:T(8,128)S(1)}) custom-call(bf16[64,1024]{1,0:T(8,128)(2,1)} %refs_0_.1, bf16[64,3072]{1,0:T(8,128)(2,1)} %refs_1_.1, s32[1,3072]{1,0:T(1,128)} %bitcast.20, s32[1,3072]{1,0:T(1,128)} %bitcast.21, s32[1,1536]{1,0:T(1,128)} %bitcast.22, ...), custom_call_target="tpu_custom_call" | custom-call | tf_op jit(solution)/shard_map/layer/pallas_call | solution.py:612
  35.3 1.0 %finish.1 = (bf16[64,1024]{1,0:T(8,128)(2,1)}, bf16[64,3072]{1,0:T(8,128)(2,1)}, f32[64,192]{1,0:T(8,128)}, f32[1,64]{1,0:T(1,128)}, f32[64,64]{1,0:T(8,128)}, /...) custom-call(bf16[64,1024]{1,0:T(8,128)(2,1)S(1)} %get-tuple-element., ...), custom_call_target="tpu_custom_call" | custom-call | tf_op jit(solution)/shard_map/finish/pallas_call | solution.py:623

commit v7 on v6

--- a/solution.py
+++ b/solution.py
@@ -144,13 +144,21 @@
                 dd = lax.rem(d + (step + 32), 32)
                 return lax.div(dd, 8), lax.rem(lax.div(dd, 2), 4), lax.rem(dd, 2), t
 
+            far = (0, 1, 2, 1)
+            a_steps = sorted(range(1, 8), key=lambda j: -2 * far[j // 2] - j % 2)
+            b_steps = sorted(range(1, 16), key=lambda j: -far[j // 4] - far[j % 4])
+
             def a_peer(j):
-                other = lax.rem(a + j, 8)
-                return other, (lax.div(other, 2), y, lax.rem(other, 2), s)
+                step = a_steps[j - 1]
+                far_z = lax.rem(z + step // 2, 4)
+                far_core = lax.rem(core + step % 2, 2)
+                return far_z * 2 + far_core, (far_z, y, far_core, s)
 
             def b_peer(j):
-                other = lax.rem(b + j, 16)
-                return other, (z, lax.div(other, 4), core, lax.rem(other, 4))
+                step = b_steps[j - 1]
+                far_y = lax.rem(y + step // 4, 4)
+                far_s = lax.rem(s + step % 4, 4)
+                return far_y * 4 + far_s, (z, far_y, core, far_s)
 
             halo_pairs = [(o, r) for o in range(3) for r in range(4) if not (o == 1 and r == 0)]
             barrier = pltpu.get_barrier_semaphore()
@@ -391,12 +399,6 @@
             scatter(i, ehd[0:64, at], col_s[at, :], gac, range(4, 10), i == 0)
 
         staged([sum_ghosts], NF // BLK)
-        def sum_senders(i):
-            at = block_at(i)
-            scatter(i, ehd[0:64, at], col_s[at, :], acc, range(4), i == 0)
-
-        staged([sum_senders], NF // BLK)
-
         def split_vectors(total):
             lane = lax.broadcasted_iota(jnp.int32, (32, 128), 1)
             whole = total + pltpu.roll(total, 122, 1)
@@ -442,6 +444,12 @@
             if comm:
                 for k in (2 * pair, 2 * pair + 1):
                     backward.append(send_block(k, gsend, gback, (sem_bs, sem_br), -1))
+
+        def sum_senders(i):
+            at = block_at(i)
+            scatter(i, ehd[0:64, at], col_s[at, :], acc, range(4), i == 0)
+
+        staged([sum_senders], NF // BLK)
 
         def sum_receivers(i):
             at = block_at(i)

time: 36.6 us -> 35.7 us (0.975)
  Pallas kernels: 35.6 us -> 34.9 us
    pallas_call x1, Pallas kernels: 34.7 us -> 34 us  [call(): pl.pallas_call(make_kernel(comm), out_shape=[jax.ShapeDtypeStruct(shape,...]
where the time goes in v7:
time: 35.7 us; the launch traced here: 35.6 us
  Pallas kernels  34.9 us (98%)
  between operations  0.66 us (2%)
    pallas_call x1, Pallas kernels, call(): pl.pallas_call(make_kernel(comm), out_shape=[jax.ShapeDtypeStruct(shape,...  34 us
    pallas_call x1, Pallas kernels, call(): pl.pallas_call(finish, out_shape=[jax.ShapeDtypeStruct(shape, kind) for s...  0.96 us

profile of v7, /device:TPU:1, one launch (start us, length us, event | category | flops | bytes accessed | tf_op | source)
XLA Modules:
  0.0 35.6 jit_solution(459682244030255226)
XLA Ops:
  0.7 34.0 %layer.1 = (bf16[64,1024]{1,0:T(8,128)(2,1)S(1)}, bf16[64,3072]{1,0:T(8,128)(2,1)S(1)}, f32[256,128]{1,0:T(8,128)S(1)}) custom-call(bf16[64,1024]{1,0:T(8,128)(2,1)} %refs_0_.1, bf16[64,3072]{1,0:T(8,128)(2,1)} %refs_1_.1, s32[1,3072]{1,0:T(1,128)} %bitcast.20, s32[1,3072]{1,0:T(1,128)} %bitcast.21, s32[1,1536]{1,0:T(1,128)} %bitcast.22, ...), custom_call_target="tpu_custom_call" | custom-call | tf_op jit(solution)/shard_map/layer/pallas_call | solution.py:620
  34.6 1.0 %finish.1 = (bf16[64,1024]{1,0:T(8,128)(2,1)}, bf16[64,3072]{1,0:T(8,128)(2,1)}, f32[64,192]{1,0:T(8,128)}, f32[1,64]{1,0:T(1,128)}, f32[64,64]{1,0:T(8,128)}, /...) custom-call(bf16[64,1024]{1,0:T(8,128)(2,1)S(1)} %get-tuple-element., ...), custom_call_target="tpu_custom_call" | custom-call | tf_op jit(solution)/shard_map/finish/pallas_call | solution.py:631
